TPU v7x, 32 devices: a whole 2x2x4 slice. The times are simulated.
32 devices in a mesh: grp: 8 (over z, y), mem: 4 (over x, core).
Axes of the slice: x: 2, y: 2, z: 4, core: 2. Of those that a mesh axis runs over, the one named last changes fastest.
Arguments:
- queries: bfloat16 [8192, 2048], P(('grp', 'mem')), may hold values from -6 to 6
- keys: bfloat16 [8192, 2048], P(('grp', 'mem')), may hold values from -6 to 6
- values: bfloat16 [8192, 2048], P(('grp', 'mem')), may hold values from -6 to 6
- grad_out: bfloat16 [8192, 2048], P(('grp', 'mem')), may hold values from -0.125 to 0.125
- log_decay: float32 [8, 8192], P(None, ('grp', 'mem')), may hold values from -1.6 to 0
Outputs:
- grad_queries: bfloat16 [8192, 2048], P(('grp', 'mem'))
- grad_keys: bfloat16 [8192, 2048], P(('grp', 'mem'))
- grad_values: bfloat16 [8192, 2048], P(('grp', 'mem'))
All inputs are finite; a program needn't handle non-finite values.
Results may differ from a plain program's by a relative error of at most 0.0052.
Values sent between devices are 32-bit elements; how exact they have to be, the bound alone decides.
A program may use at most 128 MiB of HBM per device.

v0:
```python
import functools

import jax
import jax.numpy as jnp
from jax import lax
from jax.experimental import pallas as pl
from jax.experimental.pallas import tpu as pltpu
from jax.sharding import PartitionSpec as P

HEAD_COUNT = 8
DK = 256
DV = 256
BLOCK = 128
CORES = 2
LAG = 3
MESH = pl.DeviceIdType.MESH
F32 = jnp.float32
BF16 = jnp.bfloat16


def dot(a, b, ca, cb):
    return lax.dot_general(a, b, (((ca,), (cb,)), ((), ())), preferred_element_type=F32)


def spread_rows(row):
    flat = jnp.broadcast_to(row, (BLOCK, BLOCK))
    return flat, flat.T


def wide(mat, width):
    return jnp.concatenate([mat] * (width // BLOCK), axis=1)


def retention_kernel(
    nx, ny, nz, logs_ref, q_hbm, k_hbm, v_hbm, g_hbm, gq_ref, gk_ref, gv_ref,
    q_ref, k_ref, v_ref, g_ref, s_in, cum, local, inner, total_buf, from_buf,
    peer_buf, chip_buf, plane_buf, out_buf, ztot, zbuf, acc, ret_buf, back_buf,
    d_ref, dpeer, dchip, dplane, dtot, dz,
    s_core, r_core, s_plane, r_plane, s_z, r_z, s_ret, r_ret, s_back, r_back,
    s_dc, r_dc, s_dp, r_dp, s_dz, r_dz,
):
    count = logs_ref.shape[1] // BLOCK
    scale = DK ** (-0.5)
    chips = nx * ny
    half = HEAD_COUNT // CORES
    width = DK // chips
    chunks = [(d, k) for k in range(half) for d in range(2)]
    grp, mem = lax.axis_index("grp"), lax.axis_index("mem")
    z, y = grp // ny, lax.rem(grp, ny)
    x, core = mem // CORES, lax.rem(mem, CORES)
    chip = y * nx + x
    mate = (grp, x * CORES + 1 - core)

    def chip_id(c):
        return (z * ny + c // nx, lax.rem(c, nx) * CORES + core)

    def z_id(to):
        return (to * ny + y, mem)

    others = [lax.rem(chip + off, chips) for off in range(1, chips)]
    zs = [lax.rem(z + off, nz) for off in range(1, nz)]
    peers = [mate] + [chip_id(c) for c in others] + [z_id(t) for t in zs]
    barrier = pltpu.get_barrier_semaphore()
    for peer in peers:
        pl.semaphore_signal(barrier, inc=1, device_id=peer, device_id_type=MESH)

    def copy(src, dst, send, recv, device):
        return pltpu.make_async_remote_copy(
            src_ref=src, dst_ref=dst, send_sem=send, recv_sem=recv,
            device_id=device, device_id_type=MESH,
        )

    sent = []

    def go(*args):
        c = copy(*args)
        c.start()
        sent.append(c)

    mine, theirs = core * half, (1 - core) * half

    def block(c):
        return pl.ds(pl.multiple_of(c * width, width), width)

    def cols_of(head, size):
        return pl.ds(pl.multiple_of(head * size, size), size)

    def tokens_of(b):
        return pl.ds(b * BLOCK, BLOCK)

    def load(i, head):
        far, near = ((q_hbm, q_ref), (k_hbm, k_ref), (v_hbm, v_ref), (g_hbm, g_ref))[i]
        part = cols_of(head, DK)
        return pltpu.make_async_copy(far.at[:, part], near.at[:, part], s_in.at[i, head])

    for k in range(half):
        for head in (theirs + k, mine + k):
            for i in range(4):
                load(i, head).start()

    carried = None
    for b in range(count):
        row = logs_ref[:, b * BLOCK:(b + 1) * BLOCK]
        lane = lax.broadcasted_iota(jnp.int32, row.shape, 1)
        step = 1
        while step < BLOCK:
            row = row + jnp.where(lane >= step, pltpu.roll(row, step, 1), 0.0)
            step *= 2
        whole = jnp.exp(row[:, BLOCK - 1:BLOCK])
        carried = whole if carried is None else carried * whole
        for h in range(HEAD_COUNT):
            cum[b, h] = row[h:h + 1, :]
    carried = jnp.broadcast_to(carried, (HEAD_COUNT, DV))
    for h in range(HEAD_COUNT):
        d_ref[h] = carried[h:h + 1, :]

    def factors(head, b):
        row = cum[b, head]
        flat, cols = spread_rows(row)
        end = row[:, BLOCK - 1:BLOCK]
        return flat, cols, end

    def totals(head):
        for i in range(4):
            load(i, head).wait()
        forward = None
        reverse = []
        for b in range(count):
            _, cols, end = factors(head, b)
            kd = k_ref[tokens_of(b), cols_of(head, DK)].astype(F32) * wide(jnp.exp(end - cols), DK)
            qd = q_ref[tokens_of(b), cols_of(head, DK)].astype(F32) * wide(jnp.exp(cols), DK)
            whole = jnp.broadcast_to(jnp.exp(end), (1, DV))
            part = dot(kd.astype(BF16), v_ref[tokens_of(b), cols_of(head, DV)], 0, 0)
            if b > 0:
                local[0, b - 1, head] = forward
            forward = part if forward is None else whole * forward + part
            reverse.append(
                (whole, dot(qd.astype(BF16), g_ref[tokens_of(b), cols_of(head, DV)], 0, 0))
            )
        back = None
        for b in reversed(range(count)):
            whole, part = reverse[b]
            if b < count - 1:
                local[1, b, head] = back
            back = part if back is None else whole * back + part
        total_buf[0, head] = forward
        total_buf[1, head] = back

    lower = lax.broadcasted_iota(jnp.int32, (BLOCK, BLOCK), 0) >= lax.broadcasted_iota(
        jnp.int32, (BLOCK, BLOCK), 1
    )

    def intra(head):
        for b in range(count):
            flat, cols, _ = factors(head, b)
            decay = jnp.where(lower, jnp.exp(jnp.where(lower, cols - flat, 0.0)), 0.0)
            q = q_ref[tokens_of(b), cols_of(head, DK)]
            k = k_ref[tokens_of(b), cols_of(head, DK)]
            v = v_ref[tokens_of(b), cols_of(head, DV)]
            g = g_ref[tokens_of(b), cols_of(head, DV)]
            wg = (dot(g, v, 1, 1) * decay).astype(BF16)
            wv = (dot(q, k, 1, 1) * decay).astype(BF16)
            inner[0, head, tokens_of(b), :] = dot(wg, k, 1, 0)
            inner[1, head, tokens_of(b), :] = dot(wg, q, 0, 0)
            inner[2, head, tokens_of(b), :] = dot(wv, g, 0, 0)

    def outer(d, head):
        coming = from_buf[d, head]
        weight = None
        order = range(count) if d == 0 else range(count - 1, -1, -1)
        for step, b in enumerate(order):
            _, cols, end = factors(head, b)
            if step == 0:
                low = coming.astype(BF16)
            else:
                low = (local[d, b - 1 if d == 0 else b, head] + weight * coming).astype(BF16)
            whole = jnp.broadcast_to(jnp.exp(end), (1, DV))
            weight = whole if weight is None else weight * whole
            if d == 0:
                g = g_ref[tokens_of(b), cols_of(head, DV)]
                far = wide(jnp.exp(cols), DK) * dot(g, low, 1, 1)
                near = inner[0, head, tokens_of(b), :]
                gq_ref[tokens_of(b), cols_of(head, DK)] = (scale * (near + far)).astype(BF16)
            else:
                tail = wide(jnp.exp(end - cols), DK)
                k = k_ref[tokens_of(b), cols_of(head, DK)]
                v = v_ref[tokens_of(b), cols_of(head, DV)]
                near = inner[1, head, tokens_of(b), :]
                far = tail * dot(v, low, 1, 1)
                gk_ref[tokens_of(b), cols_of(head, DK)] = (scale * (near + far)).astype(BF16)
                near = inner[2, head, tokens_of(b), :]
                far = tail * dot(k, low, 1, 0)
                gv_ref[tokens_of(b), cols_of(head, DV)] = (scale * (near + far)).astype(BF16)

    first = core == 0

    def join_cores(n, d, j):
        copy(peer_buf.at[d, j], peer_buf.at[d, j], s_core.at[n], r_core.at[n], mate).wait_recv()
        own_d = d_ref[mine + j]
        peer_d = dpeer[mine + j]
        one = jnp.ones_like(own_d)
        if d == 0:
            w_own, w_peer = jnp.where(first, peer_d, one), jnp.where(first, one, own_d)
        else:
            w_own, w_peer = jnp.where(first, one, peer_d), jnp.where(first, own_d, one)
        chip_buf[d, j] = w_own * total_buf[d, mine + j] + w_peer * peer_buf[d, j]
        plane_buf[chip, d, j] = chip_buf[d, j, block(chip), :]
        for o in others:
            go(chip_buf.at[d, j, block(o), :], plane_buf.at[chip, d, j],
               s_plane.at[o, n], r_plane.at[chip, n], chip_id(o))

    for k in range(half):
        totals(theirs + k)
        if k == 0:
            pl.semaphore_wait(barrier, len(peers))
            go(d_ref, dpeer, s_dc, r_dc, mate)
        for d in range(2):
            n = chunks.index((d, k))
            go(total_buf.at[d, theirs + k], peer_buf.at[d, k], s_core.at[n], r_core.at[n], mate)
        totals(mine + k)
        if k == 0:
            copy(d_ref, dpeer, s_dc, r_dc, mate).wait_recv()
            dchip[...] = d_ref[...] * dpeer[...]
            dplane[chip] = d_ref[...] * dpeer[...]
            for o in others:
                go(dchip, dplane.at[chip], s_dp.at[o], r_dp.at[chip], chip_id(o))
        for d in range(2):
            join_cores(chunks.index((d, k)), d, k)

    for o in others:
        copy(dchip, dplane.at[o], s_dp.at[o], r_dp.at[o], chip_id(o)).wait_recv()
    total = dplane[0]
    for c in range(1, chips):
        total = total * dplane[c]
    dtot[...] = total
    for t in zs:
        go(dtot, dz.at[z], s_dz.at[t], r_dz.at[z], z_id(t))

    def add_planes(n, d, j):
        acc[...] = jnp.zeros((width, DV), F32)
        for t in range(nz) if d == 0 else range(nz - 1, -1, -1):
            @pl.when((t < z) if d == 0 else (t > z))
            def _():
                copy(zbuf.at[t, d, j], zbuf.at[t, d, j],
                     s_z.at[t, n], r_z.at[t, n], z_id(t)).wait_recv()
                acc[...] = dz[t, mine + j] * acc[...] + zbuf[t, d, j]
        held = acc[...]
        weight = jnp.ones((1, DV), F32)
        for c in range(chips) if d == 0 else range(chips - 1, -1, -1):
            out_buf[c, d, j] = out_buf[c, d, j] + weight * held
            weight = weight * dplane[c, mine + j]
        ret_buf[d, j, block(chip), :] = out_buf[chip, d, j]
        for o in others:
            go(out_buf.at[o, d, j], ret_buf.at[d, j, block(chip), :],
               s_ret.at[o, n], r_ret.at[chip, n], chip_id(o))

    zsent = []
    for n, (d, j) in enumerate(chunks):
        for o in others:
            copy(plane_buf.at[o, d, j], plane_buf.at[o, d, j],
                 s_plane.at[o, n], r_plane.at[o, n], chip_id(o)).wait_recv()
        running = jnp.zeros((width, DV), F32)
        for c in range(chips) if d == 0 else range(chips - 1, -1, -1):
            out_buf[c, d, j] = running
            running = dplane[c, mine + j] * running + plane_buf[c, d, j]
        ztot[d, j] = running
        for t in zs:
            c = copy(ztot.at[d, j], zbuf.at[z, d, j],
                     s_z.at[t, n], r_z.at[z, n], z_id(t))
            needs = (t > z) if d == 0 else (t < z)
            pl.when(needs)(c.start)
            zsent.append((needs, c))
        for h in range(n, HEAD_COUNT, len(chunks)):
            intra(h)
        if n == LAG - 1:
            for t in zs:
                copy(dtot, dz.at[t], s_dz.at[t], r_dz.at[t], z_id(t)).wait_recv()
        if n >= LAG:
            add_planes(n - LAG, *chunks[n - LAG])
    for n in range(len(chunks) - LAG, len(chunks)):
        add_planes(n, *chunks[n])

    def finish(n, d, j):
        copy(back_buf.at[d, j], from_buf.at[d, theirs + j],
             s_back.at[n], r_back.at[n], mate).wait_recv()
        outer(d, theirs + j)

    for n, (d, j) in enumerate(chunks):
        for o in others:
            copy(out_buf.at[o, d, j], ret_buf.at[d, j, block(o), :],
                 s_ret.at[o, n], r_ret.at[o, n], chip_id(o)).wait_recv()
        near = first if d == 0 else jnp.logical_not(first)

        @pl.when(near)
        def _():
            got = ret_buf[d, j]
            from_buf[d, mine + j] = got
            back_buf[d, j] = d_ref[mine + j] * got + total_buf[d, mine + j]

        @pl.when(jnp.logical_not(near))
        def _():
            got = ret_buf[d, j]
            back_buf[d, j] = got
            from_buf[d, mine + j] = dpeer[mine + j] * got + peer_buf[d, j]

        go(back_buf.at[d, j], from_buf.at[d, mine + j], s_back.at[n], r_back.at[n], mate)
        outer(d, mine + j)
        if n > 0:
            finish(n - 1, *chunks[n - 1])
    finish(len(chunks) - 1, *chunks[-1])
    for c in sent:
        c.wait_send()
    for needs, c in zsent:
        pl.when(needs)(c.wait_send)


def body(nx, ny, nz, queries, keys, values, grad_out, log_decay):
    tokens = queries.shape[0]
    count = tokens // BLOCK
    chips = nx * ny
    half = HEAD_COUNT // CORES
    width = DK // chips
    n = 2 * half
    vm = pl.BlockSpec(memory_space=pltpu.VMEM)
    dma = pltpu.SemaphoreType.DMA
    both = pltpu.VMEM((2, half, DK, DV), F32)
    full = pltpu.VMEM((2, HEAD_COUNT, DK, DV), F32)
    rows = pltpu.VMEM((HEAD_COUNT, 1, DV), F32)
    tok = pltpu.VMEM((tokens, HEAD_COUNT * DK), BF16)
    out = jax.ShapeDtypeStruct((tokens, HEAD_COUNT * DK), BF16)
    return pl.pallas_call(
        functools.partial(retention_kernel, nx, ny, nz),
        out_shape=(out, out, out),
        in_specs=[vm] + [pl.BlockSpec(memory_space=pltpu.HBM)] * 4,
        out_specs=(vm, vm, vm),
        scratch_shapes=[
            tok, tok, tok, tok, dma((4, HEAD_COUNT)),
            pltpu.VMEM((count, HEAD_COUNT, 1, BLOCK), F32),
            pltpu.VMEM((2, max(1, count - 1), HEAD_COUNT, DK, DV), F32),
            pltpu.VMEM((3, HEAD_COUNT, tokens, DK), F32),
            full, full,
            both, both,
            pltpu.VMEM((chips, 2, half, width, DV), F32),
            pltpu.VMEM((chips, 2, half, width, DV), F32),
            pltpu.VMEM((2, half, width, DV), F32),
            pltpu.VMEM((nz, 2, half, width, DV), F32),
            pltpu.VMEM((width, DV), F32),
            both, both,
            rows, rows, rows,
            pltpu.VMEM((chips, HEAD_COUNT, 1, DV), F32),
            rows,
            pltpu.VMEM((nz, HEAD_COUNT, 1, DV), F32),
            dma((n,)), dma((n,)),
            dma((chips, n)), dma((chips, n)),
            dma((nz, n)), dma((nz, n)),
            dma((chips, n)), dma((chips, n)),
            dma((n,)), dma((n,)),
            dma, dma,
            dma((chips,)), dma((chips,)),
            dma((nz,)), dma((nz,)),
        ],
        compiler_params=pltpu.CompilerParams(collective_id=0, has_side_effects=True, vmem_limit_bytes=50 << 20),
        name="retention",
    )(log_decay, queries, keys, values, grad_out)


def solution(mesh):
    nx = mesh.shape["mem"] // CORES
    ny = nx if mesh.shape["grp"] % nx == 0 else 1
    nz = mesh.shape["grp"] // ny
    tokens = P(("grp", "mem"), None)
    return jax.shard_map(
        functools.partial(body, nx, ny, nz),
        mesh=mesh,
        in_specs=(tokens, tokens, tokens, tokens, P(None, ("grp", "mem"))),
        out_specs=(tokens, tokens, tokens),
        check_vma=False,
    )
```

profile of v0, /device:TPU:0, one launch (start us, length us, event | category | flops | bytes accessed | tf_op | source)
XLA Modules:
  0.0 62.8 jit_solution(7580326535346804355)
XLA Ops:
  0.6 0.0 copy-start
  0.6 0.7 %copy-done = f32[8,256]{1,0:T(8,128)S(1)} copy-done((f32[8,256]{1,0:T(8,128)S(1)}, f32[8,256]{1,0:T(8,128)}, u32[]{:S(2)}) %copy-start) | copy-done | bytes 8216
  1.3 58.5 %retention.1 = (bf16[256,2048]{1,0:T(8,128)(2,1)S(1)}, bf16[256,2048]{1,0:T(8,128)(2,1)S(1)}, bf16[256,2048]{1,0:T(8,128)(2,1)S(1)}) custom-call(f32[8,256]{1,0:T(8,128)S(1)} %copy-done, bf16[256,2048]{1,0:T(8,128)(2,1)} %q_hbm.1, bf16[256,2048]{1,0:T(8,128)(2,1)} %k_hbm.1, bf16[256,2048]{1,0:T(8,128)(2,1)} %v_hbm.1, bf16[256,2048]{1,0:T(8,128)(2,1)} %g_hbm.1), custom_call_target="tpu_custom_call" | custom-call | tf_op jit(solution)/shard_map/retention/pallas_call | solution.py:331
  59.8 1.0 %copy.11 = bf16[256,2048]{1,0:T(8,128)(2,1)} copy(bf16[256,2048]{1,0:T(8,128)(2,1)S(1)} %get-tuple-element.6) | data formatting | bytes 2097152
  60.8 1.0 %copy.12 = bf16[256,2048]{1,0:T(8,128)(2,1)} copy(bf16[256,2048]{1,0:T(8,128)(2,1)S(1)} %get-tuple-element.7) | data formatting | bytes 2097152
  61.8 1.0 %copy.13 = bf16[256,2048]{1,0:T(8,128)(2,1)} copy(bf16[256,2048]{1,0:T(8,128)(2,1)S(1)} %get-tuple-element.8) | data formatting | bytes 2097152
Async XLA Ops:
  0.6 0.7 %copy-start = (f32[8,256]{1,0:T(8,128)S(1)}, f32[8,256]{1,0:T(8,128)}, u32[]{:S(2)}) copy-start(f32[8,256]{1,0:T(8,128)} %logs_ref.1) | copy-start | bytes 24580
where the time goes:
time: 63 us; the launch traced here: 62.8 us
  Pallas kernels  58.5 us (93%)
  local copies, waits for them, and re-layouts  3.6 us (6%)
  between operations  0.65 us (1%)
    pallas_call x1, Pallas kernels, body(): pl.pallas_call(functools.partial(retention_kernel, nx, ny, nz), out_shape...  58.5 us
    unnamed x5, local copies, waits for them, and re-layouts  3.6 us

commit v1 on v0

v1 whole, which is shorter than its diff:
```python
import functools

import jax
import jax.numpy as jnp
from jax import lax
from jax.experimental import pallas as pl
from jax.experimental.pallas import tpu as pltpu
from jax.sharding import PartitionSpec as P

HEAD_COUNT = 8
DK = 256
DV = 256
BLOCK = 128
CORES = 2
KEYS, VALUES, QUERIES, GRADS = range(4)
MESH = pl.DeviceIdType.MESH
F32 = jnp.float32
BF16 = jnp.bfloat16


def dot(a, b, ca, cb):
    return lax.dot_general(a, b, (((ca,), (cb,)), ((), ())), preferred_element_type=F32)


def spread_rows(row):
    flat = jnp.broadcast_to(row, (BLOCK, BLOCK))
    return flat, flat.T


def wide(mat, width):
    return jnp.concatenate([mat] * (width // BLOCK), axis=1)


def retention_kernel(
    nx, ny, nz, logs_hbm, q_hbm, k_hbm, v_hbm, g_hbm, gq_ref, gk_ref, gv_ref,
    logs_ref, toks, cum, local, inner, total_buf, from_buf, peer_buf, back_buf,
    chip_buf, x_in, row_tot, y_in, plane_tot, z_in, acc, y_out, row_carry, x_out, carry,
    d_core, d_mate, d_x, d_y, d_z,
    s_logs, s_in, s_core, r_core, s_x, r_x, s_y, r_y, s_z, r_z,
    s_yout, r_yout, s_xout, r_xout, s_back, r_back, s_d, r_d,
):
    count = logs_ref.shape[1] // BLOCK
    scale = DK ** (-0.5)
    half = HEAD_COUNT // CORES
    wx = DK // nx
    wy = wx // ny
    chunks = [(d, k) for k in range(half) for d in range(2)]
    grp, mem = lax.axis_index("grp"), lax.axis_index("mem")
    z, y = grp // ny, lax.rem(grp, ny)
    x, core = mem // CORES, lax.rem(mem, CORES)
    mate = (grp, x * CORES + 1 - core)

    def x_id(to):
        return (grp, to * CORES + core)

    def y_id(to):
        return (z * ny + to, mem)

    def z_id(to):
        return (to * ny + y, mem)

    xs = [lax.rem(x + off, nx) for off in range(1, nx)]
    ys = [lax.rem(y + off, ny) for off in range(1, ny)]
    zs = [lax.rem(z + off, nz) for off in range(1, nz)]
    peers = [mate] + [x_id(o) for o in xs] + [y_id(o) for o in ys] + [z_id(o) for o in zs]
    barrier = pltpu.get_barrier_semaphore()
    for peer in peers:
        pl.semaphore_signal(barrier, inc=1, device_id=peer, device_id_type=MESH)

    def copy(src, dst, send, recv, device):
        return pltpu.make_async_remote_copy(
            src_ref=src, dst_ref=dst, send_sem=send, recv_sem=recv,
            device_id=device, device_id_type=MESH,
        )

    def go(*args):
        copy(*args).start()

    def landed(ref, sem):
        copy(ref, ref, s_back, sem, mate).wait_recv()

    def left(ref, sem):
        copy(ref, ref, sem, r_back.at[0], mate).wait_send()

    def members(d, size):
        return range(size) if d == 0 else range(size - 1, -1, -1)

    mine, theirs = core * half, (1 - core) * half

    def rows_of(c, size):
        return pl.ds(pl.multiple_of(c * size, size), size)

    def cols_of(head, size):
        return pl.ds(pl.multiple_of(head * size, size), size)

    def tokens_of(b):
        return pl.ds(b * BLOCK, BLOCK)

    load_logs = pltpu.make_async_copy(logs_hbm, logs_ref, s_logs)
    load_logs.start()
    for k in range(half):
        for head in (theirs + k, mine + k):
            part = cols_of(head, DK)
            for i, far in enumerate((k_hbm, v_hbm, q_hbm, g_hbm)):
                pltpu.make_async_copy(
                    far.at[:, part], toks.at[i, :, part], s_in.at[i // 2, head]
                ).start()

    def ready(pair, head):
        held = toks.at[pl.ds(2 * pair, 2), :, cols_of(head, DK)]
        pltpu.make_async_copy(held, held, s_in.at[pair, head]).wait()

    def tok(i, head, b):
        return toks[i, tokens_of(b), cols_of(head, DK)]

    load_logs.wait()
    carried = None
    for b in range(count):
        row = logs_ref[:, b * BLOCK:(b + 1) * BLOCK]
        lane = lax.broadcasted_iota(jnp.int32, row.shape, 1)
        step = 1
        while step < BLOCK:
            row = row + jnp.where(lane >= step, pltpu.roll(row, step, 1), 0.0)
            step *= 2
        whole = jnp.exp(row[:, BLOCK - 1:BLOCK])
        carried = whole if carried is None else carried * whole
        for h in range(HEAD_COUNT):
            cum[b, h] = row[h:h + 1, :]
    carried = jnp.broadcast_to(carried, (HEAD_COUNT, DV))
    for h in range(HEAD_COUNT):
        d_core[h] = carried[h:h + 1, :]

    def factors(head, b):
        row = cum[b, head]
        flat, cols = spread_rows(row)
        end = row[:, BLOCK - 1:BLOCK]
        return flat, cols, end

    def forward_total(head):
        ready(0, head)
        forward = None
        for b in range(count):
            _, cols, end = factors(head, b)
            kd = tok(KEYS, head, b).astype(F32) * wide(jnp.exp(end - cols), DK)
            whole = jnp.broadcast_to(jnp.exp(end), (1, DV))
            part = dot(kd.astype(BF16), tok(VALUES, head, b), 0, 0)
            if b > 0:
                local[0, b - 1, head] = forward
            forward = part if forward is None else whole * forward + part
        total_buf[0, head] = forward

    def reverse_total(head):
        ready(1, head)
        back = None
        for b in reversed(range(count)):
            _, cols, end = factors(head, b)
            qd = tok(QUERIES, head, b).astype(F32) * wide(jnp.exp(cols), DK)
            whole = jnp.broadcast_to(jnp.exp(end), (1, DV))
            part = dot(qd.astype(BF16), tok(GRADS, head, b), 0, 0)
            if b < count - 1:
                local[1, b, head] = back
            back = part if back is None else whole * back + part
        total_buf[1, head] = back

    lower = lax.broadcasted_iota(jnp.int32, (BLOCK, BLOCK), 0) >= lax.broadcasted_iota(
        jnp.int32, (BLOCK, BLOCK), 1
    )

    def intra(head):
        for b in range(count):
            flat, cols, _ = factors(head, b)
            decay = jnp.where(lower, jnp.exp(jnp.where(lower, cols - flat, 0.0)), 0.0)
            q, k = tok(QUERIES, head, b), tok(KEYS, head, b)
            v, g = tok(VALUES, head, b), tok(GRADS, head, b)
            wg = (dot(g, v, 1, 1) * decay).astype(BF16)
            wv = (dot(q, k, 1, 1) * decay).astype(BF16)
            inner[0, head, tokens_of(b), :] = dot(wg, k, 1, 0)
            inner[1, head, tokens_of(b), :] = dot(wg, q, 0, 0)
            inner[2, head, tokens_of(b), :] = dot(wv, g, 0, 0)

    def outer(d, head):
        coming = from_buf[d, head]
        weight = None
        for step, b in enumerate(members(d, count)):
            _, cols, end = factors(head, b)
            if step == 0:
                low = coming.astype(BF16)
            else:
                low = (local[d, b - 1 if d == 0 else b, head] + weight * coming).astype(BF16)
            whole = jnp.broadcast_to(jnp.exp(end), (1, DV))
            weight = whole if weight is None else weight * whole
            if d == 0:
                far = wide(jnp.exp(cols), DK) * dot(tok(GRADS, head, b), low, 1, 1)
                near = inner[0, head, tokens_of(b), :]
                gq_ref[tokens_of(b), cols_of(head, DK)] = (scale * (near + far)).astype(BF16)
            else:
                tail = wide(jnp.exp(end - cols), DK)
                near = inner[1, head, tokens_of(b), :]
                far = tail * dot(tok(VALUES, head, b), low, 1, 1)
                gk_ref[tokens_of(b), cols_of(head, DK)] = (scale * (near + far)).astype(BF16)
                near = inner[2, head, tokens_of(b), :]
                far = tail * dot(tok(KEYS, head, b), low, 1, 0)
                gv_ref[tokens_of(b), cols_of(head, DV)] = (scale * (near + far)).astype(BF16)

    first = core == 0

    def send_core(n, d, j):
        go(total_buf.at[d, theirs + j], peer_buf.at[d, j], s_core, r_core.at[n], mate)

    def join_cores(n, d, j):
        landed(peer_buf.at[d, j], r_core.at[n])
        own_d, peer_d = d_core[mine + j], d_mate[mine + j]
        one = jnp.ones_like(own_d)
        if d == 0:
            w_own, w_peer = jnp.where(first, peer_d, one), jnp.where(first, one, own_d)
        else:
            w_own, w_peer = jnp.where(first, one, peer_d), jnp.where(first, own_d, one)
        chip_buf[d, j] = w_own * total_buf[d, mine + j] + w_peer * peer_buf[d, j]
        for o in xs:
            go(chip_buf.at[d, j, rows_of(o, wx), :], x_in.at[x, d, j], s_x, r_x.at[n], x_id(o))
        x_in[x, d, j] = chip_buf[d, j, rows_of(x, wx), :]

    def fold(d, j, parts, decays, size):
        running = None
        for c in members(d, size):
            part = parts[c, d, j]
            running = part if running is None else decays[c, mine + j] * running + part
        return running

    def up_x(n, d, j):
        if n == 0:
            landed(d_x.at[pl.ds(0, nx - 1)], r_d.at[1])
            product = d_x[0]
            for c in range(1, nx):
                product = product * d_x[c]
            d_y[y] = product
            for o in ys:
                go(d_y.at[y], d_y.at[y], s_d.at[2], r_d.at[2], y_id(o))
        landed(x_in.at[pl.ds(0, nx - 1), d, j], r_x.at[n])
        row_tot[d, j] = fold(d, j, x_in, d_x, nx)
        for o in ys:
            go(row_tot.at[d, j, rows_of(o, wy), :], y_in.at[y, d, j], s_y, r_y.at[n], y_id(o))
        y_in[y, d, j] = row_tot[d, j, rows_of(y, wy), :]

    def up_y(n, d, j):
        if n == 0:
            if ny > 1:
                landed(d_y.at[pl.ds(0, ny - 1)], r_d.at[2])
            product = d_y[0]
            for c in range(1, ny):
                product = product * d_y[c]
            d_z[z] = product
            for t in zs:
                go(d_z.at[z], d_z.at[z], s_d.at[3], r_d.at[3], z_id(t))
        if ny > 1:
            landed(y_in.at[pl.ds(0, ny - 1), d, j], r_y.at[n])
        plane_tot[d, j] = fold(d, j, y_in, d_y, ny)
        for t in zs:
            c = copy(plane_tot.at[d, j], z_in.at[z, d, j], s_z, r_z.at[z, n], z_id(t))
            pl.when((t > z) if d == 0 else (t < z))(c.start)

    def spread(d, j, held, parts, decays, size, out):
        last = members(d, size)[-1]
        for c in members(d, size):
            out[c, d, j] = held
            if c != last:
                held = decays[c, mine + j] * held + parts[c, d, j]

    def over_z(n, d, j):
        if n == 0 and nz > 1:
            landed(d_z.at[pl.ds(0, nz - 1)], r_d.at[3])
        acc[...] = jnp.zeros((wy, DV), F32)
        for t in members(d, nz):
            @pl.when((t < z) if d == 0 else (t > z))
            def _():
                landed(z_in.at[t, d, j], r_z.at[t, n])
                acc[...] = d_z[t, mine + j] * acc[...] + z_in[t, d, j]
        spread(d, j, acc[...], y_in, d_y, ny, y_out)

    def send_y(n, d, j):
        for o in ys:
            go(y_out.at[o, d, j], row_carry.at[d, j, rows_of(y, wy), :], s_yout, r_yout.at[n], y_id(o))
        row_carry[d, j, rows_of(y, wy), :] = y_out[y, d, j]

    def down_y(n, d, j):
        if ny > 1:
            landed(row_carry.at[d, j, pl.ds(0, (ny - 1) * wy), :], r_yout.at[n])
        spread(d, j, row_carry[d, j], x_in, d_x, nx, x_out)
        for o in xs:
            go(x_out.at[o, d, j], carry.at[d, j, rows_of(x, wx), :], s_xout, r_xout.at[n], x_id(o))
        carry[d, j, rows_of(x, wx), :] = x_out[x, d, j]

    def down_x(n, d, j):
        landed(carry.at[d, j, pl.ds(0, (nx - 1) * wx), :], r_xout.at[n])
        near = first if d == 0 else jnp.logical_not(first)

        @pl.when(near)
        def _():
            got = carry[d, j]
            back_buf[d, j] = d_core[mine + j] * got + total_buf[d, mine + j]
            from_buf[d, mine + j] = got

        @pl.when(jnp.logical_not(near))
        def _():
            got = carry[d, j]
            back_buf[d, j] = got
            from_buf[d, mine + j] = d_mate[mine + j] * got + peer_buf[d, j]

        go(back_buf.at[d, j], from_buf.at[d, mine + j], s_back, r_back.at[n], mate)
        outer(d, mine + j)

    def finish(n, d, j):
        landed(from_buf.at[d, theirs + j], r_back.at[n])
        outer(d, theirs + j)

    todo = []
    for k in range(half):
        todo += [
            (forward_total, theirs + k, 2 * k), (reverse_total, theirs + k, 2 * k + 1),
            (forward_total, mine + k, None), (reverse_total, mine + k, None),
        ]
    after = {}
    for n in range(len(chunks)):
        after[min(4 * (n // 2) + 4 + n % 2, len(todo) - 1 + n % 2)] = n
    for i, (work, head, n) in enumerate(todo):
        work(head)
        if i == 0:
            pl.semaphore_wait(barrier, len(peers))
            go(d_core, d_mate, s_d.at[0], r_d.at[0], mate)
        if n is not None:
            send_core(n, *chunks[n])
        if i in after:
            m = after[i]
            if m == 0:
                landed(d_mate, r_d.at[0])
                d_x[x] = d_core[...] * d_mate[...]
                for o in xs:
                    go(d_x.at[x], d_x.at[x], s_d.at[1], r_d.at[1], x_id(o))
            join_cores(m, *chunks[m])
    for i in sorted(after):
        if i >= len(todo):
            join_cores(after[i], *chunks[after[i]])

    stages = ((0, up_x), (1, up_y), (3, over_z), (3, send_y), (4, down_y))
    for slot in range(len(chunks) + 4):
        for lag, stage in stages:
            n = slot - lag
            if 0 <= n < len(chunks):
                stage(n, *chunks[n])
            if lag == 0:
                for h in range(slot, HEAD_COUNT, len(chunks)) if slot < len(chunks) else ():
                    intra(h)
    for n, (d, j) in enumerate(chunks):
        down_x(n, d, j)
        if n > 0:
            finish(n - 1, *chunks[n - 1])
    finish(len(chunks) - 1, *chunks[-1])

    left(peer_buf, s_core)
    left(x_in.at[pl.ds(0, nx - 1)], s_x)
    left(x_out.at[pl.ds(0, nx - 1)], s_xout)
    left(back_buf, s_back)
    left(d_mate, s_d.at[0])
    left(d_x.at[pl.ds(0, nx - 1)], s_d.at[1])
    if ny > 1:
        left(y_in.at[pl.ds(0, ny - 1)], s_y)
        left(y_out.at[pl.ds(0, ny - 1)], s_yout)
        left(d_y.at[pl.ds(0, ny - 1)], s_d.at[2])
    if nz > 1:
        left(z_in.at[pl.ds(0, nz - 1), 0], s_z)
        left(d_z.at[pl.ds(0, nz - 1)], s_d.at[3])


def write_kernel(gq_ref, gk_ref, gv_ref, gq_hbm, gk_hbm, gv_hbm, sems):
    copies = [
        pltpu.make_async_copy(near, far, sems.at[i])
        for i, (near, far) in enumerate(((gq_ref, gq_hbm), (gk_ref, gk_hbm), (gv_ref, gv_hbm)))
    ]
    for c in copies:
        c.start()
    for c in copies:
        c.wait()


def body(nx, ny, nz, queries, keys, values, grad_out, log_decay):
    tokens = queries.shape[0]
    count = tokens // BLOCK
    half = HEAD_COUNT // CORES
    wx = DK // nx
    wy = wx // ny
    n = 2 * half
    vm = pl.BlockSpec(memory_space=pltpu.VMEM)
    hbm = pl.BlockSpec(memory_space=pltpu.HBM)
    dma = pltpu.SemaphoreType.DMA

    def states(*lead):
        return pltpu.VMEM(lead + (DV,), F32)

    def decays(*lead):
        return pltpu.VMEM(lead + (HEAD_COUNT, 1, DV), F32)

    out = jax.ShapeDtypeStruct((tokens, HEAD_COUNT * DK), BF16)
    grads = pl.pallas_call(
        functools.partial(retention_kernel, nx, ny, nz),
        out_shape=(out, out, out),
        in_specs=[hbm] * 5,
        out_specs=(vm, vm, vm),
        scratch_shapes=[
            pltpu.VMEM((HEAD_COUNT, tokens), F32),
            pltpu.VMEM((4, tokens, HEAD_COUNT * DK), BF16),
            pltpu.VMEM((count, HEAD_COUNT, 1, BLOCK), F32),
            states(2, max(1, count - 1), HEAD_COUNT, DK),
            states(3, HEAD_COUNT, tokens),
            states(2, HEAD_COUNT, DK), states(2, HEAD_COUNT, DK),
            states(2, half, DK), states(2, half, DK),
            states(2, half, DK), states(nx, 2, half, wx), states(2, half, wx),
            states(ny, 2, half, wy), states(2, half, wy), states(nz, 2, half, wy), states(wy),
            states(ny, 2, half, wy), states(2, half, wx),
            states(nx, 2, half, wx), states(2, half, DK),
            decays(), decays(), decays(nx), decays(ny), decays(nz),
            dma, dma((2, HEAD_COUNT)),
            dma, dma((n,)), dma, dma((n,)), dma, dma((n,)), dma, dma((nz, n)),
            dma, dma((n,)), dma, dma((n,)), dma, dma((n,)), dma((4,)), dma((4,)),
        ],
        compiler_params=pltpu.CompilerParams(collective_id=0, has_side_effects=True, vmem_limit_bytes=52 << 20),
        name="retention",
    )(log_decay, queries, keys, values, grad_out)
    return pl.pallas_call(
        write_kernel,
        out_shape=(out, out, out),
        in_specs=[vm] * 3,
        out_specs=(hbm, hbm, hbm),
        scratch_shapes=[dma((3,))],
        name="write",
    )(*grads)


def solution(mesh):
    nx = mesh.shape["mem"] // CORES
    ny = nx if mesh.shape["grp"] % nx == 0 else 1
    nz = mesh.shape["grp"] // ny
    tokens = P(("grp", "mem"), None)
    return jax.shard_map(
        functools.partial(body, nx, ny, nz),
        mesh=mesh,
        in_specs=(tokens, tokens, tokens, tokens, P(None, ("grp", "mem"))),
        out_specs=(tokens, tokens, tokens),
        check_vma=False,
    )
```

time: 63 us -> 63.8 us (1.013)
  the two profiles are of different devices: /device:TPU:0 before, /device:TPU:1 now
where the time goes in v1:
time: 63.8 us; the launch traced here: 63.6 us
  Pallas kernels  61.3 us (96%)
  local copies, waits for them, and re-layouts  1.68 us (3%)
  between operations  0.66 us (1%)
    pallas_call x1, Pallas kernels, body(): pl.pallas_call(functools.partial(retention_kernel, nx, ny, nz), out_shape...  57.8 us
    pallas_call x1, Pallas kernels, body(): pl.pallas_call(write_kernel, out_shape=(out, out, out), in_specs=[vm] * 3...  3.54 us
    unnamed x4, local copies, waits for them, and re-layouts  1.68 us

profile of v1, /device:TPU:1, one launch (start us, length us, event | category | flops | bytes accessed | tf_op | source)
XLA Modules:
  0.0 63.6 jit_solution(9026586499690874347)
XLA Ops:
  0.6 0.0 copy-start.1
  0.6 0.7 %copy-done.1 = f32[8,256]{1,0:T(8,128)S(1)} copy-done((f32[8,256]{1,0:T(8,128)S(1)}, f32[8,256]{1,0:T(8,128)}, u32[]{:S(2)}) %copy-start.1) | copy-done | bytes 8216
  1.3 57.8 %retention.1 = (bf16[256,2048]{1,0:T(8,128)(2,1)S(1)}, bf16[256,2048]{1,0:T(8,128)(2,1)}, bf16[256,2048]{1,0:T(8,128)(2,1)}) custom-call(f32[8,256]{1,0:T(8,128)S(1)} %copy-done.1, bf16[256,2048]{1,0:T(8,128)(2,1)} %q_hbm.1, bf16[256,2048]{1,0:T(8,128)(2,1)} %k_hbm.1, bf16[256,2048]{1,0:T(8,128)(2,1)} %v_hbm.1, bf16[256,2048]{1,0:T(8,128)(2,1)} %g_hbm.1), custom_call_target="tpu_custom_call" | custom-call | tf_op jit(solution)/shard_map/retention/pallas_call | solution.py:403
  59.1 0.0 copy-start
  59.1 1.0 %copy-done = bf16[256,2048]{1,0:T(8,128)(2,1)} copy-done((bf16[256,2048]{1,0:T(8,128)(2,1)}, bf16[256,2048]{1,0:T(8,128)(2,1)S(1)}, u32[]{:S(2)}) %copy-start) | copy-done | bytes 1048600
  60.1 3.5 %write.1 = (bf16[256,2048]{1,0:T(8,128)(2,1)}, bf16[256,2048]{1,0:T(8,128)(2,1)}, bf16[256,2048]{1,0:T(8,128)(2,1)}) custom-call(bf16[256,2048]{1,0:T(8,128)(2,1)} %copy-done, bf16[256,2048]{1,0:T(8,128)(2,1)} %get-tuple-element.7.gk_ref, bf16[256,2048]{1,0:T(8,128)(2,1)} %get-tuple-element.8.gv_ref), custom_call_target="tpu_custom_call" | custom-call | tf_op jit(solution)/shard_map/write/pallas_call | solution.py:428
Async XLA Ops:
  0.6 0.7 %copy-start.1 = (f32[8,256]{1,0:T(8,128)S(1)}, f32[8,256]{1,0:T(8,128)}, u32[]{:S(2)}) copy-start(f32[8,256]{1,0:T(8,128)} %logs_hbm.1) | copy-start | bytes 24580
  59.1 1.0 %copy-start = (bf16[256,2048]{1,0:T(8,128)(2,1)}, bf16[256,2048]{1,0:T(8,128)(2,1)S(1)}, u32[]{:S(2)}) copy-start(bf16[256,2048]{1,0:T(8,128)(2,1)S(1)} %get-tuple-element.6.gq_ref) | copy-start | bytes 3145732

commit v2 on v1

--- a/solution.py
+++ b/solution.py
@@ -35,8 +35,7 @@
     nx, ny, nz, logs_hbm, q_hbm, k_hbm, v_hbm, g_hbm, gq_ref, gk_ref, gv_ref,
     logs_ref, toks, cum, local, inner, total_buf, from_buf, peer_buf, back_buf,
     chip_buf, x_in, row_tot, y_in, plane_tot, z_in, acc, y_out, row_carry, x_out, carry,
-    d_core, d_mate, d_x, d_y, d_z,
-    s_logs, s_in, s_core, r_core, s_x, r_x, s_y, r_y, s_z, r_z,
+    decay_rows, s_meet, s_logs, s_in, s_core, r_core, s_x, r_x, s_y, r_y, s_z, r_z,
     s_yout, r_yout, s_xout, r_xout, s_back, r_back, s_d, r_d,
 ):
     count = logs_ref.shape[1] // BLOCK
@@ -44,6 +43,9 @@
     half = HEAD_COUNT // CORES
     wx = DK // nx
     wy = wx // ny
+    d_core, d_mate = decay_rows.at[0], decay_rows.at[1]
+    d_x, d_y = decay_rows.at[pl.ds(2, nx)], decay_rows.at[pl.ds(2 + nx, ny)]
+    d_z = decay_rows.at[pl.ds(2 + nx + ny, nz)]
     chunks = [(d, k) for k in range(half) for d in range(2)]
     grp, mem = lax.axis_index("grp"), lax.axis_index("mem")
     z, y = grp // ny, lax.rem(grp, ny)
@@ -62,10 +64,26 @@
     xs = [lax.rem(x + off, nx) for off in range(1, nx)]
     ys = [lax.rem(y + off, ny) for off in range(1, ny)]
     zs = [lax.rem(z + off, nz) for off in range(1, nz)]
-    peers = [mate] + [x_id(o) for o in xs] + [y_id(o) for o in ys] + [z_id(o) for o in zs]
     barrier = pltpu.get_barrier_semaphore()
-    for peer in peers:
-        pl.semaphore_signal(barrier, inc=1, device_id=peer, device_id_type=MESH)
+
+    def tell(sem, device):
+        pl.semaphore_signal(sem, inc=1, device_id=device, device_id_type=MESH)
+
+    for device in [(grp, o * CORES) for o in xs] + [(z * ny + o, x * CORES) for o in ys]:
+        tell(barrier, device)
+    pl.when(core == 1)(lambda: tell(barrier, mate))
+    for o in zs:
+        tell(barrier, (o * ny + y, x * CORES + 1))
+
+    def meet(hearer, signals):
+        @pl.when(core == hearer)
+        def _():
+            pl.semaphore_wait(barrier, signals)
+            tell(s_meet, mate)
+
+        @pl.when(core != hearer)
+        def _():
+            pl.semaphore_wait(s_meet, 1)
 
     def copy(src, dst, send, recv, device):
         return pltpu.make_async_remote_copy(
@@ -99,16 +117,17 @@
     load_logs = pltpu.make_async_copy(logs_hbm, logs_ref, s_logs)
     load_logs.start()
     for k in range(half):
-        for head in (theirs + k, mine + k):
+        for side, head in enumerate((theirs + k, mine + k)):
             part = cols_of(head, DK)
             for i, far in enumerate((k_hbm, v_hbm, q_hbm, g_hbm)):
+                slot = k + 3 if k else 2 * side + i // 2
                 pltpu.make_async_copy(
-                    far.at[:, part], toks.at[i, :, part], s_in.at[i // 2, head]
+                    far.at[:, part], toks.at[i, :, part], s_in.at[slot]
                 ).start()
 
-    def ready(pair, head):
-        held = toks.at[pl.ds(2 * pair, 2), :, cols_of(head, DK)]
-        pltpu.make_async_copy(held, held, s_in.at[pair, head]).wait()
+    def ready(k, slot):
+        held = toks.at[:, :, pl.ds(0, CORES * DK)] if k else toks.at[pl.ds(0, 2), :, pl.ds(0, DK)]
+        pltpu.make_async_copy(held, held, s_in.at[slot]).wait()
 
     def tok(i, head, b):
         return toks[i, tokens_of(b), cols_of(head, DK)]
@@ -137,7 +156,6 @@
         return flat, cols, end
 
     def forward_total(head):
-        ready(0, head)
         forward = None
         for b in range(count):
             _, cols, end = factors(head, b)
@@ -150,7 +168,6 @@
         total_buf[0, head] = forward
 
     def reverse_total(head):
-        ready(1, head)
         back = None
         for b in reversed(range(count)):
             _, cols, end = factors(head, b)
@@ -235,7 +252,7 @@
                 product = product * d_x[c]
             d_y[y] = product
             for o in ys:
-                go(d_y.at[y], d_y.at[y], s_d.at[2], r_d.at[2], y_id(o))
+                go(d_y.at[y], d_y.at[y], s_d, r_d.at[2], y_id(o))
         landed(x_in.at[pl.ds(0, nx - 1), d, j], r_x.at[n])
         row_tot[d, j] = fold(d, j, x_in, d_x, nx)
         for o in ys:
@@ -250,13 +267,15 @@
             for c in range(1, ny):
                 product = product * d_y[c]
             d_z[z] = product
+            if nz > 1:
+                meet(1, CORES * (nz - 1))
             for t in zs:
-                go(d_z.at[z], d_z.at[z], s_d.at[3], r_d.at[3], z_id(t))
+                go(d_z.at[z], d_z.at[z], s_d, r_d.at[3], z_id(t))
         if ny > 1:
             landed(y_in.at[pl.ds(0, ny - 1), d, j], r_y.at[n])
         plane_tot[d, j] = fold(d, j, y_in, d_y, ny)
         for t in zs:
-            c = copy(plane_tot.at[d, j], z_in.at[z, d, j], s_z, r_z.at[z, n], z_id(t))
+            c = copy(plane_tot.at[d, j], z_in.at[z, d, j], s_z, r_z.at[n], z_id(t))
             pl.when((t > z) if d == 0 else (t < z))(c.start)
 
     def spread(d, j, held, parts, decays, size, out):
@@ -270,10 +289,13 @@
         if n == 0 and nz > 1:
             landed(d_z.at[pl.ds(0, nz - 1)], r_d.at[3])
         acc[...] = jnp.zeros((wy, DV), F32)
+        for coming in range(1, nz):
+            @pl.when((z if d == 0 else nz - 1 - z) == coming)
+            def _():
+                landed(z_in.at[pl.ds(0, coming), d, j], r_z.at[n])
         for t in members(d, nz):
             @pl.when((t < z) if d == 0 else (t > z))
             def _():
-                landed(z_in.at[t, d, j], r_z.at[t, n])
                 acc[...] = d_z[t, mine + j] * acc[...] + z_in[t, d, j]
         spread(d, j, acc[...], y_in, d_y, ny, y_out)
 
@@ -321,12 +343,16 @@
         ]
     after = {}
     for n in range(len(chunks)):
-        after[min(4 * (n // 2) + 4 + n % 2, len(todo) - 1 + n % 2)] = n
+        after[min(4 * (n // 2) + 3 + n % 2, len(todo) - 1 + n % 2)] = n
     for i, (work, head, n) in enumerate(todo):
+        if i < 4:
+            ready(0, i)
+        elif i % 4 == 0:
+            ready(i // 4, i // 4 + 3)
         work(head)
         if i == 0:
-            pl.semaphore_wait(barrier, len(peers))
-            go(d_core, d_mate, s_d.at[0], r_d.at[0], mate)
+            meet(0, 1 + CORES * (nx + ny - 2))
+            go(d_core, d_mate, s_d, r_d.at[0], mate)
         if n is not None:
             send_core(n, *chunks[n])
         if i in after:
@@ -335,7 +361,7 @@
                 landed(d_mate, r_d.at[0])
                 d_x[x] = d_core[...] * d_mate[...]
                 for o in xs:
-                    go(d_x.at[x], d_x.at[x], s_d.at[1], r_d.at[1], x_id(o))
+                    go(d_x.at[x], d_x.at[x], s_d, r_d.at[1], x_id(o))
             join_cores(m, *chunks[m])
     for i in sorted(after):
         if i >= len(todo):
@@ -360,15 +386,12 @@
     left(x_in.at[pl.ds(0, nx - 1)], s_x)
     left(x_out.at[pl.ds(0, nx - 1)], s_xout)
     left(back_buf, s_back)
-    left(d_mate, s_d.at[0])
-    left(d_x.at[pl.ds(0, nx - 1)], s_d.at[1])
+    left(decay_rows.at[pl.ds(0, nx + ny + nz - 2)], s_d)
     if ny > 1:
         left(y_in.at[pl.ds(0, ny - 1)], s_y)
         left(y_out.at[pl.ds(0, ny - 1)], s_yout)
-        left(d_y.at[pl.ds(0, ny - 1)], s_d.at[2])
     if nz > 1:
         left(z_in.at[pl.ds(0, nz - 1), 0], s_z)
-        left(d_z.at[pl.ds(0, nz - 1)], s_d.at[3])
 
 
 def write_kernel(gq_ref, gk_ref, gv_ref, gq_hbm, gk_hbm, gv_hbm, sems):
@@ -400,9 +423,10 @@
         return pltpu.VMEM(lead + (HEAD_COUNT, 1, DV), F32)
 
     out = jax.ShapeDtypeStruct((tokens, HEAD_COUNT * DK), BF16)
+    near = pltpu.VMEM(out.shape, out.dtype)
     grads = pl.pallas_call(
         functools.partial(retention_kernel, nx, ny, nz),
-        out_shape=(out, out, out),
+        out_shape=(near, near, near),
         in_specs=[hbm] * 5,
         out_specs=(vm, vm, vm),
         scratch_shapes=[
@@ -417,14 +441,13 @@
             states(ny, 2, half, wy), states(2, half, wy), states(nz, 2, half, wy), states(wy),
             states(ny, 2, half, wy), states(2, half, wx),
             states(nx, 2, half, wx), states(2, half, DK),
-            decays(), decays(), decays(nx), decays(ny), decays(nz),
-            dma, dma((2, HEAD_COUNT)),
-            dma, dma((n,)), dma, dma((n,)), dma, dma((n,)), dma, dma((nz, n)),
-            dma, dma((n,)), dma, dma((n,)), dma, dma((n,)), dma((4,)), dma((4,)),
+            decays(2 + nx + ny + nz), pltpu.SemaphoreType.REGULAR, dma, dma((half + 3,)),
+            dma, dma((n,)), dma, dma((n,)), dma, dma((n,)), dma, dma((n,)),
+            dma, dma((n,)), dma, dma((n,)), dma, dma((n,)), dma, dma((4,)),
         ],
         compiler_params=pltpu.CompilerParams(collective_id=0, has_side_effects=True, vmem_limit_bytes=52 << 20),
         name="retention",
-    )(log_decay, queries, keys, values, grad_out)
+    )(pltpu.with_memory_space_constraint(log_decay, pltpu.HBM), queries, keys, values, grad_out)
     return pl.pallas_call(
         write_kernel,
         out_shape=(out, out, out),
@@ -432,7 +455,7 @@
         out_specs=(hbm, hbm, hbm),
         scratch_shapes=[dma((3,))],
         name="write",
-    )(*grads)
+    )(*(pltpu.with_memory_space_constraint(g, pltpu.VMEM) for g in grads))
 
 
 def solution(mesh):

time: 63.8 us -> 58.2 us (0.912)
  the two profiles are of different devices: /device:TPU:1 before, /device:TPU:29 now
where the time goes in v2:
time: 58.2 us; the launch traced here: 57.2 us
  Pallas kernels  56.6 us (97%)
  between operations  0.64 us (1%)
    pallas_call x1, Pallas kernels, body(): pl.pallas_call(functools.partial(retention_kernel, nx, ny, nz), out_shape...  54.9 us
    pallas_call x1, Pallas kernels, body(): pl.pallas_call(write_kernel, out_shape=(out, out, out), in_specs=[vm] * 3...  1.69 us

profile of v2, /device:TPU:29, one launch (start us, length us, event | category | flops | bytes accessed | tf_op | source)
XLA Modules:
  0.0 57.2 jit_solution(11239369122635124318)
XLA Ops:
  0.6 54.9 %retention.1 = (bf16[256,2048]{1,0:T(8,128)(2,1)S(1)}, bf16[256,2048]{1,0:T(8,128)(2,1)S(1)}, bf16[256,2048]{1,0:T(8,128)(2,1)S(1)}) custom-call(f32[8,256]{1,0:T(8,128)} %logs_hbm.1, bf16[256,2048]{1,0:T(8,128)(2,1)} %q_hbm.1, bf16[256,2048]{1,0:T(8,128)(2,1)} %k_hbm.1, bf16[256,2048]{1,0:T(8,128)(2,1)} %v_hbm.1, bf16[256,2048]{1,0:T(8,128)(2,1)} %g_hbm.1), custom_call_target="tpu_custom_call" | custom-call | tf_op jit(solution)/shard_map/retention/pallas_call | solution.py:427
  55.5 1.7 %write.1 = (bf16[256,2048]{1,0:T(8,128)(2,1)}, bf16[256,2048]{1,0:T(8,128)(2,1)}, bf16[256,2048]{1,0:T(8,128)(2,1)}) custom-call(bf16[256,2048]{1,0:T(8,128)(2,1)S(1)} %get-tuple-element.6.gq_ref, bf16[256,2048]{1,0:T(8,128)(2,1)S(1)} %get-tuple-element.7.gk_ref, bf16[256,2048]{1,0:T(8,128)(2,1)S(1)} %get-tuple-element.8.gv_ref), custom_call_target="tpu_custom_call" | custom-call | tf_op jit(solution)/shard_map/write/pallas_call | solution.py:451

commit v3 on v2

--- a/solution.py
+++ b/solution.py
@@ -34,8 +34,8 @@
 def retention_kernel(
     nx, ny, nz, logs_hbm, q_hbm, k_hbm, v_hbm, g_hbm, gq_ref, gk_ref, gv_ref,
     logs_ref, toks, cum, local, inner, total_buf, from_buf, peer_buf, back_buf,
-    chip_buf, x_in, row_tot, y_in, plane_tot, z_in, acc, y_out, row_carry, x_out, carry,
-    decay_rows, s_meet, s_logs, s_in, s_core, r_core, s_x, r_x, s_y, r_y, s_z, r_z,
+    chip_buf, x_in, row_tot, y_in, plane_tot, z_in, z_out, z_carry, y_out, row_carry, x_out, carry,
+    decay_rows, weights, s_meet, s_logs, s_in, s_core, r_core, r_first, s_x, r_x, s_y, r_y, s_z, r_z,
     s_yout, r_yout, s_xout, r_xout, s_back, r_back, s_d, r_d,
 ):
     count = logs_ref.shape[1] // BLOCK
@@ -75,12 +75,13 @@
     for o in zs:
         tell(barrier, (o * ny + y, x * CORES + 1))
 
-    def meet(hearer, signals):
+    def hear(hearer, signals):
         @pl.when(core == hearer)
         def _():
             pl.semaphore_wait(barrier, signals)
             tell(s_meet, mate)
 
+    def learn(hearer):
         @pl.when(core != hearer)
         def _():
             pl.semaphore_wait(s_meet, 1)
@@ -116,7 +117,8 @@
 
     load_logs = pltpu.make_async_copy(logs_hbm, logs_ref, s_logs)
     load_logs.start()
-    for k in range(half):
+
+    def load(k):
         for side, head in enumerate((theirs + k, mine + k)):
             part = cols_of(head, DK)
             for i, far in enumerate((k_hbm, v_hbm, q_hbm, g_hbm)):
@@ -125,6 +127,8 @@
                     far.at[:, part], toks.at[i, :, part], s_in.at[slot]
                 ).start()
 
+    load(0)
+
     def ready(k, slot):
         held = toks.at[:, :, pl.ds(0, CORES * DK)] if k else toks.at[pl.ds(0, 2), :, pl.ds(0, DK)]
         pltpu.make_async_copy(held, held, s_in.at[slot]).wait()
@@ -132,22 +136,24 @@
     def tok(i, head, b):
         return toks[i, tokens_of(b), cols_of(head, DK)]
 
+    square = (BLOCK, BLOCK)
+    lower = lax.broadcasted_iota(jnp.int32, square, 0) >= lax.broadcasted_iota(jnp.int32, square, 1)
+    ones = jnp.where(lower, 1.0, 0.0)
     load_logs.wait()
     carried = None
     for b in range(count):
-        row = logs_ref[:, b * BLOCK:(b + 1) * BLOCK]
-        lane = lax.broadcasted_iota(jnp.int32, row.shape, 1)
-        step = 1
-        while step < BLOCK:
-            row = row + jnp.where(lane >= step, pltpu.roll(row, step, 1), 0.0)
-            step *= 2
+        row = lax.dot_general(
+            logs_ref[:, b * BLOCK:(b + 1) * BLOCK], ones, (((1,), (1,)), ((), ())),
+            precision=lax.Precision.HIGHEST, preferred_element_type=F32,
+        )
+        for h in range(HEAD_COUNT):
+            cum[b, h] = row[h:h + 1, :]
         whole = jnp.exp(row[:, BLOCK - 1:BLOCK])
         carried = whole if carried is None else carried * whole
-        for h in range(HEAD_COUNT):
-            cum[b, h] = row[h:h + 1, :]
     carried = jnp.broadcast_to(carried, (HEAD_COUNT, DV))
     for h in range(HEAD_COUNT):
         d_core[h] = carried[h:h + 1, :]
+    hear(0, 1 + CORES * (nx + ny - 2))
 
     def factors(head, b):
         row = cum[b, head]
@@ -178,10 +184,6 @@
                 local[1, b, head] = back
             back = part if back is None else whole * back + part
         total_buf[1, head] = back
-
-    lower = lax.broadcasted_iota(jnp.int32, (BLOCK, BLOCK), 0) >= lax.broadcasted_iota(
-        jnp.int32, (BLOCK, BLOCK), 1
-    )
 
     def intra(head):
         for b in range(count):
@@ -222,20 +224,36 @@
     first = core == 0
 
     def send_core(n, d, j):
-        go(total_buf.at[d, theirs + j], peer_buf.at[d, j], s_core, r_core.at[n], mate)
+        if n:
+            go(total_buf.at[d, theirs + j], peer_buf.at[d, j], s_core, r_core.at[n], mate)
+        else:
+            for i, o in enumerate(xs + [x]):
+                part = rows_of(o, wx)
+                go(total_buf.at[d, theirs + j, part, :], peer_buf.at[d, j, part, :],
+                   s_core, r_first.at[i], mate)
 
     def join_cores(n, d, j):
-        landed(peer_buf.at[d, j], r_core.at[n])
+        if n:
+            landed(peer_buf.at[d, j], r_core.at[n])
         own_d, peer_d = d_core[mine + j], d_mate[mine + j]
         one = jnp.ones_like(own_d)
         if d == 0:
             w_own, w_peer = jnp.where(first, peer_d, one), jnp.where(first, one, own_d)
         else:
             w_own, w_peer = jnp.where(first, one, peer_d), jnp.where(first, own_d, one)
-        chip_buf[d, j] = w_own * total_buf[d, mine + j] + w_peer * peer_buf[d, j]
-        for o in xs:
+
+        def joined(o):
+            part = rows_of(o, wx)
+            return w_own * total_buf[d, mine + j, part, :] + w_peer * peer_buf[d, j, part, :]
+
+        for i, o in enumerate(xs):
+            if n == 0:
+                landed(peer_buf.at[d, j, rows_of(o, wx), :], r_first.at[i])
+            chip_buf[d, j, rows_of(o, wx), :] = joined(o)
             go(chip_buf.at[d, j, rows_of(o, wx), :], x_in.at[x, d, j], s_x, r_x.at[n], x_id(o))
-        x_in[x, d, j] = chip_buf[d, j, rows_of(x, wx), :]
+        if n == 0:
+            landed(peer_buf.at[d, j, rows_of(x, wx), :], r_first.at[nx - 1])
+        x_in[x, d, j] = joined(x)
 
     def fold(d, j, parts, decays, size):
         running = None
@@ -268,15 +286,44 @@
                 product = product * d_y[c]
             d_z[z] = product
             if nz > 1:
-                meet(1, CORES * (nz - 1))
+                hear(1, CORES * (nz - 1))
+                learn(1)
             for t in zs:
                 go(d_z.at[z], d_z.at[z], s_d, r_d.at[3], z_id(t))
         if ny > 1:
             landed(y_in.at[pl.ds(0, ny - 1), d, j], r_y.at[n])
         plane_tot[d, j] = fold(d, j, y_in, d_y, ny)
-        for t in zs:
-            c = copy(plane_tot.at[d, j], z_in.at[z, d, j], s_z, r_z.at[n], z_id(t))
-            pl.when((t > z) if d == 0 else (t < z))(c.start)
+        send_z(n, d, j, 0, plane_tot.at[d, j])
+
+    levels = (nz - 1).bit_length()
+
+    def place(d):
+        return z if d == 0 else nz - 1 - z
+
+    def z_sends(d, level):
+        size, p = 1 << level, place(d)
+        last = lax.rem(p, 2 * size) == size - 1
+        return [(i + 1, jnp.logical_and(last, p + i + 1 < nz)) for i in range(size)]
+
+    def z_hears(d, level):
+        return lax.rem(place(d), 2 << level) >= 1 << level
+
+    def send_z(n, d, j, level, src):
+        if level < levels:
+            for hop, needed in z_sends(d, level):
+                to = lax.rem(z + hop, nz) if d == 0 else lax.rem(z - hop + nz, nz)
+                c = copy(src, z_in.at[2 * level + d, j], s_z, r_z.at[level, n], z_id(to))
+                pl.when(needed)(c.start)
+
+    def z_weight(d, level):
+        size = 1 << level
+        start = place(d) // size * size
+        weight = jnp.ones_like(d_core[...])
+        for i in range(size - 1):
+            q = lax.rem(start + i, nz)
+            passed = d_z[q if d == 0 else nz - 1 - q]
+            weight = jnp.where(start + i < place(d), weight * passed, weight)
+        return weight
 
     def spread(d, j, held, parts, decays, size, out):
         last = members(d, size)[-1]
@@ -285,35 +332,69 @@
             if c != last:
                 held = decays[c, mine + j] * held + parts[c, d, j]
 
-    def over_z(n, d, j):
-        if n == 0 and nz > 1:
+    def over_z(level, n, d, j):
+        if n == 0 and level == 0:
             landed(d_z.at[pl.ds(0, nz - 1)], r_d.at[3])
-        acc[...] = jnp.zeros((wy, DV), F32)
-        for coming in range(1, nz):
-            @pl.when((z if d == 0 else nz - 1 - z) == coming)
+            for side in range(2):
+                for upper in range(levels):
+                    weights[upper, side] = z_weight(side, upper)
+        if level == 0:
+            z_carry[d, j] = jnp.zeros((wy, DV), F32)
+
+        @pl.when(z_hears(d, level))
+        def _():
+            landed(z_in.at[2 * level + d, j], r_z.at[level, n])
+            came = z_in[2 * level + d, j]
+            if level:
+                came = weights[level, d, mine + j] * came + z_carry[d, j]
+            z_carry[d, j] = came
+
+        if level + 1 < levels:
+            @pl.when(z_sends(d, level + 1)[0][1])
             def _():
-                landed(z_in.at[pl.ds(0, coming), d, j], r_z.at[n])
-        for t in members(d, nz):
-            @pl.when((t < z) if d == 0 else (t > z))
-            def _():
-                acc[...] = d_z[t, mine + j] * acc[...] + z_in[t, d, j]
-        spread(d, j, acc[...], y_in, d_y, ny, y_out)
+                z_out[level, d, j] = d_z[z, mine + j] * z_carry[d, j] + plane_tot[d, j]
+
+            send_z(n, d, j, level + 1, z_out.at[level, d, j])
+
+    def down_z(n, d, j):
+        if levels:
+            over_z(levels - 1, n, d, j)
+        else:
+            z_carry[d, j] = jnp.zeros((wy, DV), F32)
+        spread(d, j, z_carry[d, j], y_in, d_y, ny, y_out)
+        send_y(n, d, j)
 
     def send_y(n, d, j):
         for o in ys:
             go(y_out.at[o, d, j], row_carry.at[d, j, rows_of(y, wy), :], s_yout, r_yout.at[n], y_id(o))
         row_carry[d, j, rows_of(y, wy), :] = y_out[y, d, j]
+
+    def starts(d, at):
+        row = jnp.logical_and(z == (0 if d == 0 else nz - 1), y == (0 if d == 0 else ny - 1))
+        return jnp.logical_and(row, at == (0 if d == 0 else nx - 1))
 
     def down_y(n, d, j):
         if ny > 1:
             landed(row_carry.at[d, j, pl.ds(0, (ny - 1) * wy), :], r_yout.at[n])
         spread(d, j, row_carry[d, j], x_in, d_x, nx, x_out)
         for o in xs:
-            go(x_out.at[o, d, j], carry.at[d, j, rows_of(x, wx), :], s_xout, r_xout.at[n], x_id(o))
+            c = copy(
+                x_out.at[o, d, j], carry.at[d, j, rows_of(x, wx), :], s_xout.at[d], r_xout.at[n], x_id(o)
+            )
+            pl.when(jnp.logical_not(starts(d, o)))(c.start)
         carry[d, j, rows_of(x, wx), :] = x_out[x, d, j]
 
     def down_x(n, d, j):
-        landed(carry.at[d, j, pl.ds(0, (nx - 1) * wx), :], r_xout.at[n])
+        starting = starts(d, x)
+
+        @pl.when(starting)
+        def _():
+            carry[d, j] = jnp.zeros((DK, DV), F32)
+
+        @pl.when(jnp.logical_not(starting))
+        def _():
+            landed(carry.at[d, j, pl.ds(0, (nx - 1) * wx), :], r_xout.at[n])
+
         near = first if d == 0 else jnp.logical_not(first)
 
         @pl.when(near)
@@ -351,8 +432,10 @@
             ready(i // 4, i // 4 + 3)
         work(head)
         if i == 0:
-            meet(0, 1 + CORES * (nx + ny - 2))
+            learn(0)
             go(d_core, d_mate, s_d, r_d.at[0], mate)
+            for k in range(1, half):
+                load(k)
         if n is not None:
             send_core(n, *chunks[n])
         if i in after:
@@ -367,31 +450,44 @@
         if i >= len(todo):
             join_cores(after[i], *chunks[after[i]])
 
-    stages = ((0, up_x), (1, up_y), (3, over_z), (3, send_y), (4, down_y))
-    for slot in range(len(chunks) + 4):
+    def inside(n, d, j):
+        for h in range(n, HEAD_COUNT, len(chunks)):
+            intra(h)
+
+    climb = [(2 + level, functools.partial(over_z, level)) for level in range(levels - 1)]
+    top = 2 + len(climb)
+    back = len(chunks)
+    stages = [(0, up_x), (0, inside), (top + 2, down_y), (back + 1, finish), (back, down_x)]
+    stages += [(1, up_y)] + climb + [(top, down_z)]
+    for slot in range(2 * len(chunks) + 1):
         for lag, stage in stages:
             n = slot - lag
             if 0 <= n < len(chunks):
                 stage(n, *chunks[n])
-            if lag == 0:
-                for h in range(slot, HEAD_COUNT, len(chunks)) if slot < len(chunks) else ():
-                    intra(h)
-    for n, (d, j) in enumerate(chunks):
-        down_x(n, d, j)
-        if n > 0:
-            finish(n - 1, *chunks[n - 1])
-    finish(len(chunks) - 1, *chunks[-1])
 
     left(peer_buf, s_core)
     left(x_in.at[pl.ds(0, nx - 1)], s_x)
-    left(x_out.at[pl.ds(0, nx - 1)], s_xout)
+    withheld = [
+        sum(jnp.where(starts(d, o), 1, 0) for o in xs) for d in range(2)
+    ]
+    for d in range(2):
+        for amount in (nx - 2, nx - 1):
+            if amount:
+                pl.when(withheld[d] == nx - 1 - amount)(
+                    functools.partial(left, x_out.at[pl.ds(0, amount), d], s_xout.at[d])
+                )
     left(back_buf, s_back)
     left(decay_rows.at[pl.ds(0, nx + ny + nz - 2)], s_d)
     if ny > 1:
         left(y_in.at[pl.ds(0, ny - 1)], s_y)
         left(y_out.at[pl.ds(0, ny - 1)], s_yout)
     if nz > 1:
-        left(z_in.at[pl.ds(0, nz - 1), 0], s_z)
+        sends = sum(
+            jnp.where(needed, 1, 0)
+            for level in range(levels) for d in range(2) for _, needed in z_sends(d, level)
+        )
+        for amount in range(1, nz):
+            pl.when(sends == amount)(functools.partial(left, z_in.at[pl.ds(0, amount)], s_z))
 
 
 def write_kernel(gq_ref, gk_ref, gv_ref, gq_hbm, gk_hbm, gv_hbm, sems):
@@ -411,6 +507,7 @@
     half = HEAD_COUNT // CORES
     wx = DK // nx
     wy = wx // ny
+    levels = (nz - 1).bit_length()
     n = 2 * half
     vm = pl.BlockSpec(memory_space=pltpu.VMEM)
     hbm = pl.BlockSpec(memory_space=pltpu.HBM)
@@ -438,12 +535,13 @@
             states(2, HEAD_COUNT, DK), states(2, HEAD_COUNT, DK),
             states(2, half, DK), states(2, half, DK),
             states(2, half, DK), states(nx, 2, half, wx), states(2, half, wx),
-            states(ny, 2, half, wy), states(2, half, wy), states(nz, 2, half, wy), states(wy),
+            states(ny, 2, half, wy), states(2, half, wy),
+            states(max(2 * levels, nz), half, wy), states(max(1, levels - 1), 2, half, wy), states(2, half, wy),
             states(ny, 2, half, wy), states(2, half, wx),
             states(nx, 2, half, wx), states(2, half, DK),
-            decays(2 + nx + ny + nz), pltpu.SemaphoreType.REGULAR, dma, dma((half + 3,)),
-            dma, dma((n,)), dma, dma((n,)), dma, dma((n,)), dma, dma((n,)),
-            dma, dma((n,)), dma, dma((n,)), dma, dma((n,)), dma, dma((4,)),
+            decays(2 + nx + ny + nz), decays(max(1, levels), 2), pltpu.SemaphoreType.REGULAR, dma, dma((half + 3,)),
+            dma, dma((n,)), dma((nx,)), dma, dma((n,)), dma, dma((n,)), dma, dma((max(1, levels), n)),
+            dma, dma((n,)), dma((2,)), dma((n,)), dma, dma((n,)), dma, dma((4,)),
         ],
         compiler_params=pltpu.CompilerParams(collective_id=0, has_side_effects=True, vmem_limit_bytes=52 << 20),
         name="retention",

time: 58.2 us -> 56.8 us (0.976)
  Pallas kernels: 56.6 us -> 55.2 us
    pallas_call x1, Pallas kernels: 54.9 us -> 53.5 us  [body(): pl.pallas_call(functools.partial(retention_kernel, nx, ny, nz), out_shape...]
where the time goes in v3:
time: 56.8 us; the launch traced here: 55.8 us
  Pallas kernels  55.2 us (97%)
  between operations  0.64 us (1%)
    pallas_call x1, Pallas kernels, body(): pl.pallas_call(functools.partial(retention_kernel, nx, ny, nz), out_shape...  53.5 us
    pallas_call x1, Pallas kernels, body(): pl.pallas_call(write_kernel, out_shape=(out, out, out), in_specs=[vm] * 3...  1.69 us

profile of v3, /device:TPU:29, one launch (start us, length us, event | category | flops | bytes accessed | tf_op | source)
XLA Modules:
  0.0 55.8 jit_solution(4435582199656739229)
XLA Ops:
  0.6 53.5 %retention.1 = (bf16[256,2048]{1,0:T(8,128)(2,1)S(1)}, bf16[256,2048]{1,0:T(8,128)(2,1)S(1)}, bf16[256,2048]{1,0:T(8,128)(2,1)S(1)}) custom-call(f32[8,256]{1,0:T(8,128)} %logs_hbm.1, bf16[256,2048]{1,0:T(8,128)(2,1)} %q_hbm.1, bf16[256,2048]{1,0:T(8,128)(2,1)} %k_hbm.1, bf16[256,2048]{1,0:T(8,128)(2,1)} %v_hbm.1, bf16[256,2048]{1,0:T(8,128)(2,1)} %g_hbm.1), custom_call_target="tpu_custom_call" | custom-call | tf_op jit(solution)/shard_map/retention/pallas_call | solution.py:524
  54.2 1.7 %write.1 = (bf16[256,2048]{1,0:T(8,128)(2,1)}, bf16[256,2048]{1,0:T(8,128)(2,1)}, bf16[256,2048]{1,0:T(8,128)(2,1)}) custom-call(bf16[256,2048]{1,0:T(8,128)(2,1)S(1)} %get-tuple-element.6.gq_ref, bf16[256,2048]{1,0:T(8,128)(2,1)S(1)} %get-tuple-element.7.gk_ref, bf16[256,2048]{1,0:T(8,128)(2,1)S(1)} %get-tuple-element.8.gv_ref), custom_call_target="tpu_custom_call" | custom-call | tf_op jit(solution)/shard_map/write/pallas_call | solution.py:549

commit v4 on v3

--- a/solution.py
+++ b/solution.py
@@ -47,6 +47,7 @@
     d_x, d_y = decay_rows.at[pl.ds(2, nx)], decay_rows.at[pl.ds(2 + nx, ny)]
     d_z = decay_rows.at[pl.ds(2 + nx + ny, nz)]
     chunks = [(d, k) for k in range(half) for d in range(2)]
+    chunks[-2:] = chunks[:-3:-1]
     grp, mem = lax.axis_index("grp"), lax.axis_index("mem")
     z, y = grp // ny, lax.rem(grp, ny)
     x, core = mem // CORES, lax.rem(mem, CORES)
@@ -118,16 +119,13 @@
     load_logs = pltpu.make_async_copy(logs_hbm, logs_ref, s_logs)
     load_logs.start()
 
-    def load(k):
-        for side, head in enumerate((theirs + k, mine + k)):
-            part = cols_of(head, DK)
-            for i, far in enumerate((k_hbm, v_hbm, q_hbm, g_hbm)):
-                slot = k + 3 if k else 2 * side + i // 2
-                pltpu.make_async_copy(
-                    far.at[:, part], toks.at[i, :, part], s_in.at[slot]
-                ).start()
-
-    load(0)
+    def load(head, pair, slot):
+        part = cols_of(head, DK)
+        for i in (2 * pair, 2 * pair + 1):
+            far = (k_hbm, v_hbm, q_hbm, g_hbm)[i]
+            pltpu.make_async_copy(far.at[:, part], toks.at[i, :, part], s_in.at[slot]).start()
+
+    load(theirs, 0, 0)
 
     def ready(k, slot):
         held = toks.at[:, :, pl.ds(0, CORES * DK)] if k else toks.at[pl.ds(0, 2), :, pl.ds(0, DK)]
@@ -140,6 +138,8 @@
     lower = lax.broadcasted_iota(jnp.int32, square, 0) >= lax.broadcasted_iota(jnp.int32, square, 1)
     ones = jnp.where(lower, 1.0, 0.0)
     load_logs.wait()
+    for slot, head in ((2, mine), (1, theirs), (3, mine)):
+        load(head, slot % 2, slot)
     carried = None
     for b in range(count):
         row = lax.dot_general(
@@ -153,8 +153,6 @@
     carried = jnp.broadcast_to(carried, (HEAD_COUNT, DV))
     for h in range(HEAD_COUNT):
         d_core[h] = carried[h:h + 1, :]
-    hear(0, 1 + CORES * (nx + ny - 2))
-
     def factors(head, b):
         row = cum[b, head]
         flat, cols = spread_rows(row)
@@ -416,39 +414,54 @@
         landed(from_buf.at[d, theirs + j], r_back.at[n])
         outer(d, theirs + j)
 
-    todo = []
-    for k in range(half):
-        todo += [
-            (forward_total, theirs + k, 2 * k), (reverse_total, theirs + k, 2 * k + 1),
-            (forward_total, mine + k, None), (reverse_total, mine + k, None),
-        ]
-    after = {}
-    for n in range(len(chunks)):
-        after[min(4 * (n // 2) + 3 + n % 2, len(todo) - 1 + n % 2)] = n
-    for i, (work, head, n) in enumerate(todo):
-        if i < 4:
-            ready(0, i)
-        elif i % 4 == 0:
-            ready(i // 4, i // 4 + 3)
-        work(head)
-        if i == 0:
-            learn(0)
-            go(d_core, d_mate, s_d, r_d.at[0], mate)
-            for k in range(1, half):
-                load(k)
-        if n is not None:
+    def load_more(k):
+        for head in (theirs + k, mine + k):
+            load(head, 0, k + 3)
+            load(head, 1, k + 3)
+
+    def greet_mate():
+        go(d_core, d_mate, s_d, r_d.at[0], mate)
+        send_core(0, *chunks[0])
+
+    totals = (forward_total, reverse_total)
+    ready(0, 0)
+    forward_total(theirs)
+    hear(0, 1 + CORES * (nx + ny - 2))
+    pl.when(core == 0)(greet_mate)
+    ready(0, 2)
+    forward_total(mine)
+    learn(0)
+    pl.when(core != 0)(greet_mate)
+    load_more(1)
+    ready(0, 1)
+    reverse_total(theirs)
+    send_core(1, *chunks[1])
+    landed(d_mate, r_d.at[0])
+    d_x[x] = d_core[...] * d_mate[...]
+    for o in xs:
+        go(d_x.at[x], d_x.at[x], s_d, r_d.at[1], x_id(o))
+    join_cores(0, *chunks[0])
+    for k in range(2, half):
+        load_more(k)
+    ready(0, 3)
+    reverse_total(mine)
+    join_cores(1, *chunks[1])
+    late = []
+    for k in range(1, half):
+        ready(k, k + 3)
+        turn = [n for n, (_, j) in enumerate(chunks) if j == k]
+        for n in turn:
+            totals[chunks[n][0]](theirs + k)
             send_core(n, *chunks[n])
-        if i in after:
-            m = after[i]
-            if m == 0:
-                landed(d_mate, r_d.at[0])
-                d_x[x] = d_core[...] * d_mate[...]
-                for o in xs:
-                    go(d_x.at[x], d_x.at[x], s_d, r_d.at[1], x_id(o))
-            join_cores(m, *chunks[m])
-    for i in sorted(after):
-        if i >= len(todo):
-            join_cores(after[i], *chunks[after[i]])
+            for m in late:
+                join_cores(m, *chunks[m])
+            late = []
+        for n in turn:
+            totals[chunks[n][0]](mine + k)
+        join_cores(turn[0], *chunks[turn[0]])
+        late = turn[1:]
+    for m in late:
+        join_cores(m, *chunks[m])
 
     def inside(n, d, j):
         for h in range(n, HEAD_COUNT, len(chunks)):
@@ -457,9 +470,9 @@
     climb = [(2 + level, functools.partial(over_z, level)) for level in range(levels - 1)]
     top = 2 + len(climb)
     back = len(chunks)
-    stages = [(0, up_x), (0, inside), (top + 2, down_y), (back + 1, finish), (back, down_x)]
+    stages = [(0, up_x), (0, inside), (top + 2, down_y), (back + 2, finish), (back, down_x)]
     stages += [(1, up_y)] + climb + [(top, down_z)]
-    for slot in range(2 * len(chunks) + 1):
+    for slot in range(2 * len(chunks) + 2):
         for lag, stage in stages:
             n = slot - lag
             if 0 <= n < len(chunks):

time: 56.8 us -> 55.7 us (0.981); the launches traced: 55.8 us -> 55.5 us
  no operation moved by 1% of the time
where the time goes in v4:
time: 55.7 us; the launch traced here: 55.5 us
  Pallas kernels  54.9 us (99%)
  between operations  0.64 us (1%)
    pallas_call x1, Pallas kernels, body(): pl.pallas_call(functools.partial(retention_kernel, nx, ny, nz), out_shape...  53.2 us
    pallas_call x1, Pallas kernels, body(): pl.pallas_call(write_kernel, out_shape=(out, out, out), in_specs=[vm] * 3...  1.69 us

profile of v4, /device:TPU:29, one launch (start us, length us, event | category | flops | bytes accessed | tf_op | source)
XLA Modules:
  0.0 55.5 jit_solution(13013337183862370466)
XLA Ops:
  0.6 53.2 %retention.1 = (bf16[256,2048]{1,0:T(8,128)(2,1)S(1)}, bf16[256,2048]{1,0:T(8,128)(2,1)S(1)}, bf16[256,2048]{1,0:T(8,128)(2,1)S(1)}) custom-call(f32[8,256]{1,0:T(8,128)} %logs_hbm.1, bf16[256,2048]{1,0:T(8,128)(2,1)} %q_hbm.1, bf16[256,2048]{1,0:T(8,128)(2,1)} %k_hbm.1, bf16[256,2048]{1,0:T(8,128)(2,1)} %v_hbm.1, bf16[256,2048]{1,0:T(8,128)(2,1)} %g_hbm.1), custom_call_target="tpu_custom_call" | custom-call | tf_op jit(solution)/shard_map/retention/pallas_call | solution.py:537
  53.8 1.7 %write.1 = (bf16[256,2048]{1,0:T(8,128)(2,1)}, bf16[256,2048]{1,0:T(8,128)(2,1)}, bf16[256,2048]{1,0:T(8,128)(2,1)}) custom-call(bf16[256,2048]{1,0:T(8,128)(2,1)S(1)} %get-tuple-element.6.gq_ref, bf16[256,2048]{1,0:T(8,128)(2,1)S(1)} %get-tuple-element.7.gk_ref, bf16[256,2048]{1,0:T(8,128)(2,1)S(1)} %get-tuple-element.8.gv_ref), custom_call_target="tpu_custom_call" | custom-call | tf_op jit(solution)/shard_map/write/pallas_call | solution.py:562

commit v5 on v4

--- a/solution.py
+++ b/solution.py
@@ -46,8 +46,9 @@
     d_core, d_mate = decay_rows.at[0], decay_rows.at[1]
     d_x, d_y = decay_rows.at[pl.ds(2, nx)], decay_rows.at[pl.ds(2 + nx, ny)]
     d_z = decay_rows.at[pl.ds(2 + nx + ny, nz)]
-    chunks = [(d, k) for k in range(half) for d in range(2)]
-    chunks[-2:] = chunks[:-3:-1]
+    early = max(1, half - 2)
+    chunks = [(d, k) for k in range(early) for d in range(2)]
+    chunks += [(d, k) for d in (1, 0) for k in range(early, half)]
     grp, mem = lax.axis_index("grp"), lax.axis_index("mem")
     z, y = grp // ny, lax.rem(grp, ny)
     x, core = mem // CORES, lax.rem(mem, CORES)
@@ -126,6 +127,7 @@
             pltpu.make_async_copy(far.at[:, part], toks.at[i, :, part], s_in.at[slot]).start()
 
     load(theirs, 0, 0)
+    load(mine, 0, 2)
 
     def ready(k, slot):
         held = toks.at[:, :, pl.ds(0, CORES * DK)] if k else toks.at[pl.ds(0, 2), :, pl.ds(0, DK)]
@@ -138,8 +140,8 @@
     lower = lax.broadcasted_iota(jnp.int32, square, 0) >= lax.broadcasted_iota(jnp.int32, square, 1)
     ones = jnp.where(lower, 1.0, 0.0)
     load_logs.wait()
-    for slot, head in ((2, mine), (1, theirs), (3, mine)):
-        load(head, slot % 2, slot)
+    load(theirs, 1, 1)
+    load(mine, 1, 3)
     carried = None
     for b in range(count):
         row = lax.dot_general(
@@ -371,15 +373,20 @@
         row = jnp.logical_and(z == (0 if d == 0 else nz - 1), y == (0 if d == 0 else ny - 1))
         return jnp.logical_and(row, at == (0 if d == 0 else nx - 1))
 
+    def send_x(n, d, j, ready=True):
+        for o in xs:
+            c = copy(
+                x_out.at[o, d, j], carry.at[d, j, rows_of(x, wx), :], s_xout.at[d], r_xout.at[n], x_id(o)
+            )
+            pl.when(jnp.logical_and(jnp.logical_not(starts(d, o)), ready))(c.start)
+
+    final = len(chunks) - 1
+
     def down_y(n, d, j):
         if ny > 1:
             landed(row_carry.at[d, j, pl.ds(0, (ny - 1) * wy), :], r_yout.at[n])
         spread(d, j, row_carry[d, j], x_in, d_x, nx, x_out)
-        for o in xs:
-            c = copy(
-                x_out.at[o, d, j], carry.at[d, j, rows_of(x, wx), :], s_xout.at[d], r_xout.at[n], x_id(o)
-            )
-            pl.when(jnp.logical_not(starts(d, o)))(c.start)
+        send_x(n, d, j, core == 0 if n == final else True)
         carry[d, j, rows_of(x, wx), :] = x_out[x, d, j]
 
     def down_x(n, d, j):
@@ -393,6 +400,8 @@
         def _():
             landed(carry.at[d, j, pl.ds(0, (nx - 1) * wx), :], r_xout.at[n])
 
+        if n == final - 1:
+            send_x(final, *chunks[final], core != 0)
         near = first if d == 0 else jnp.logical_not(first)
 
         @pl.when(near)
@@ -446,18 +455,20 @@
     ready(0, 3)
     reverse_total(mine)
     join_cores(1, *chunks[1])
-    late = []
-    for k in range(1, half):
-        ready(k, k + 3)
-        turn = [n for n, (_, j) in enumerate(chunks) if j == k]
+    late, held = [], {0}
+    for turn in (range(n, n + 2) for n in range(2, len(chunks), 2)):
         for n in turn:
-            totals[chunks[n][0]](theirs + k)
-            send_core(n, *chunks[n])
+            d, k = chunks[n]
+            if k not in held:
+                ready(k, k + 3)
+                held.add(k)
+            totals[d](theirs + k)
+            send_core(n, d, k)
             for m in late:
                 join_cores(m, *chunks[m])
             late = []
         for n in turn:
-            totals[chunks[n][0]](mine + k)
+            totals[chunks[n][0]](mine + chunks[n][1])
         join_cores(turn[0], *chunks[turn[0]])
         late = turn[1:]
     for m in late:
@@ -472,11 +483,15 @@
     back = len(chunks)
     stages = [(0, up_x), (0, inside), (top + 2, down_y), (back + 2, finish), (back, down_x)]
     stages += [(1, up_y)] + climb + [(top, down_z)]
-    for slot in range(2 * len(chunks) + 2):
+    for slot in range(2 * len(chunks) + 1):
         for lag, stage in stages:
             n = slot - lag
+            if stage is finish and n >= final - 1:
+                n = final
             if 0 <= n < len(chunks):
                 stage(n, *chunks[n])
+            if stage is finish and n == final - 2:
+                finish(final - 1, *chunks[final - 1])
 
     left(peer_buf, s_core)
     left(x_in.at[pl.ds(0, nx - 1)], s_x)

time: 55.7 us -> 55.5 us (level)
  Pallas kernels: 54.9 us -> 54.1 us
    pallas_call x1, Pallas kernels: 53.2 us -> 52.4 us  [body(): pl.pallas_call(functools.partial(retention_kernel, nx, ny, nz), out_shape...]
where the time goes in v5:
time: 55.5 us; the launch traced here: 54.8 us
  Pallas kernels  54.1 us (97%)
  between operations  0.64 us (1%)
    pallas_call x1, Pallas kernels, body(): pl.pallas_call(functools.partial(retention_kernel, nx, ny, nz), out_shape...  52.4 us
    pallas_call x1, Pallas kernels, body(): pl.pallas_call(write_kernel, out_shape=(out, out, out), in_specs=[vm] * 3...  1.69 us

profile of v5, /device:TPU:29, one launch (start us, length us, event | category | flops | bytes accessed | tf_op | source)
XLA Modules:
  0.0 54.8 jit_solution(1621386267087115640)
XLA Ops:
  0.6 52.4 %retention.1 = (bf16[256,2048]{1,0:T(8,128)(2,1)S(1)}, bf16[256,2048]{1,0:T(8,128)(2,1)S(1)}, bf16[256,2048]{1,0:T(8,128)(2,1)S(1)}) custom-call(f32[8,256]{1,0:T(8,128)} %logs_hbm.1, bf16[256,2048]{1,0:T(8,128)(2,1)} %q_hbm.1, bf16[256,2048]{1,0:T(8,128)(2,1)} %k_hbm.1, bf16[256,2048]{1,0:T(8,128)(2,1)} %v_hbm.1, bf16[256,2048]{1,0:T(8,128)(2,1)} %g_hbm.1), custom_call_target="tpu_custom_call" | custom-call | tf_op jit(solution)/shard_map/retention/pallas_call | solution.py:552
  53.1 1.7 %write.1 = (bf16[256,2048]{1,0:T(8,128)(2,1)}, bf16[256,2048]{1,0:T(8,128)(2,1)}, bf16[256,2048]{1,0:T(8,128)(2,1)}) custom-call(bf16[256,2048]{1,0:T(8,128)(2,1)S(1)} %get-tuple-element.6.gq_ref, bf16[256,2048]{1,0:T(8,128)(2,1)S(1)} %get-tuple-element.7.gk_ref, bf16[256,2048]{1,0:T(8,128)(2,1)S(1)} %get-tuple-element.8.gv_ref), custom_call_target="tpu_custom_call" | custom-call | tf_op jit(solution)/shard_map/write/pallas_call | solution.py:577

commit v6 on v5

--- a/solution.py
+++ b/solution.py
@@ -36,7 +36,7 @@
     logs_ref, toks, cum, local, inner, total_buf, from_buf, peer_buf, back_buf,
     chip_buf, x_in, row_tot, y_in, plane_tot, z_in, z_out, z_carry, y_out, row_carry, x_out, carry,
     decay_rows, weights, s_meet, s_logs, s_in, s_core, r_core, r_first, s_x, r_x, s_y, r_y, s_z, r_z,
-    s_yout, r_yout, s_xout, r_xout, s_back, r_back, s_d, r_d,
+    s_yout, r_yout, s_xout, r_xout, r_tail, s_back, r_back, s_d, r_d,
 ):
     count = logs_ref.shape[1] // BLOCK
     scale = DK ** (-0.5)
@@ -127,10 +127,9 @@
             pltpu.make_async_copy(far.at[:, part], toks.at[i, :, part], s_in.at[slot]).start()
 
     load(theirs, 0, 0)
-    load(mine, 0, 2)
-
-    def ready(k, slot):
-        held = toks.at[:, :, pl.ds(0, CORES * DK)] if k else toks.at[pl.ds(0, 2), :, pl.ds(0, DK)]
+
+    def ready(slot, parts, heads):
+        held = toks.at[pl.ds(0, parts), :, pl.ds(0, heads * DK)]
         pltpu.make_async_copy(held, held, s_in.at[slot]).wait()
 
     def tok(i, head, b):
@@ -140,8 +139,9 @@
     lower = lax.broadcasted_iota(jnp.int32, square, 0) >= lax.broadcasted_iota(jnp.int32, square, 1)
     ones = jnp.where(lower, 1.0, 0.0)
     load_logs.wait()
+    load(mine, 0, 2)
     load(theirs, 1, 1)
-    load(mine, 1, 3)
+    load(mine, 1, 1)
     carried = None
     for b in range(count):
         row = lax.dot_general(
@@ -225,7 +225,7 @@
 
     def send_core(n, d, j):
         if n:
-            go(total_buf.at[d, theirs + j], peer_buf.at[d, j], s_core, r_core.at[n], mate)
+            go(total_buf.at[d, theirs + j], peer_buf.at[d, j], s_core, r_core.at[n // 2], mate)
         else:
             for i, o in enumerate(xs + [x]):
                 part = rows_of(o, wx)
@@ -233,8 +233,10 @@
                    s_core, r_first.at[i], mate)
 
     def join_cores(n, d, j):
-        if n:
-            landed(peer_buf.at[d, j], r_core.at[n])
+        if n == 1:
+            landed(peer_buf.at[d, j], r_core.at[0])
+        elif n and n % 2 == 0:
+            landed(peer_buf.at[0, pl.ds(0, 2)], r_core.at[n // 2])
         own_d, peer_d = d_core[mine + j], d_mate[mine + j]
         one = jnp.ones_like(own_d)
         if d == 0:
@@ -296,6 +298,7 @@
         send_z(n, d, j, 0, plane_tot.at[d, j])
 
     levels = (nz - 1).bit_length()
+    shared = max(0, levels - 2)
 
     def place(d):
         return z if d == 0 else nz - 1 - z
@@ -312,7 +315,7 @@
         if level < levels:
             for hop, needed in z_sends(d, level):
                 to = lax.rem(z + hop, nz) if d == 0 else lax.rem(z - hop + nz, nz)
-                c = copy(src, z_in.at[2 * level + d, j], s_z, r_z.at[level, n], z_id(to))
+                c = copy(src, z_in.at[2 * level + d, j], s_z, r_z.at[min(level, shared), n], z_id(to))
                 pl.when(needed)(c.start)
 
     def z_weight(d, level):
@@ -341,13 +344,38 @@
         if level == 0:
             z_carry[d, j] = jnp.zeros((wy, DV), F32)
 
-        @pl.when(z_hears(d, level))
-        def _():
-            landed(z_in.at[2 * level + d, j], r_z.at[level, n])
+        def hear_z():
             came = z_in[2 * level + d, j]
             if level:
                 came = weights[level, d, mine + j] * came + z_carry[d, j]
             z_carry[d, j] = came
+
+        hears = z_hears(d, level)
+        if level == levels - 1 and level:
+            both = jnp.logical_and(hears, z_hears(d, level - 1))
+
+            @pl.when(both)
+            def _():
+                landed(z_in.at[pl.ds(0, 2), j], r_z.at[shared, n])
+                early = z_in[2 * (level - 1) + d, j]
+                if level > 1:
+                    early = weights[level - 1, d, mine + j] * early + z_carry[d, j]
+                z_carry[d, j] = early
+                hear_z()
+
+            @pl.when(jnp.logical_and(hears, jnp.logical_not(both)))
+            def _():
+                landed(z_in.at[2 * level + d, j], r_z.at[shared, n])
+                hear_z()
+        else:
+            alone = hears
+            if level == levels - 2:
+                alone = jnp.logical_and(hears, jnp.logical_not(z_hears(d, level + 1)))
+
+            @pl.when(alone)
+            def _():
+                landed(z_in.at[2 * level + d, j], r_z.at[level, n])
+                hear_z()
 
         if level + 1 < levels:
             @pl.when(z_sends(d, level + 1)[0][1])
@@ -373,51 +401,74 @@
         row = jnp.logical_and(z == (0 if d == 0 else nz - 1), y == (0 if d == 0 else ny - 1))
         return jnp.logical_and(row, at == (0 if d == 0 else nx - 1))
 
-    def send_x(n, d, j, ready=True):
+    final = len(chunks) - 1
+
+    def send_x(n, d, j, part=None, ready=True):
+        size = wx if part is None else wx // 2
+        start = 0 if part is None else part * size
+        sem = r_tail if part == 1 else r_xout.at[n]
         for o in xs:
             c = copy(
-                x_out.at[o, d, j], carry.at[d, j, rows_of(x, wx), :], s_xout.at[d], r_xout.at[n], x_id(o)
+                x_out.at[o, d, j, pl.ds(start, size), :],
+                carry.at[d, j, pl.ds(pl.multiple_of(x * wx + start, size), size), :],
+                s_xout.at[d], sem, x_id(o),
             )
             pl.when(jnp.logical_and(jnp.logical_not(starts(d, o)), ready))(c.start)
-
-    final = len(chunks) - 1
 
     def down_y(n, d, j):
         if ny > 1:
             landed(row_carry.at[d, j, pl.ds(0, (ny - 1) * wy), :], r_yout.at[n])
         spread(d, j, row_carry[d, j], x_in, d_x, nx, x_out)
-        send_x(n, d, j, core == 0 if n == final else True)
+        if n == final:
+            for part in range(2):
+                send_x(n, d, j, part, core == 0)
+        else:
+            send_x(n, d, j)
         carry[d, j, rows_of(x, wx), :] = x_out[x, d, j]
+        if n == final:
+            send_back(n, d, j, rows_of(x, wx))
 
     def down_x(n, d, j):
         starting = starts(d, x)
 
-        @pl.when(starting)
-        def _():
-            carry[d, j] = jnp.zeros((DK, DV), F32)
-
-        @pl.when(jnp.logical_not(starting))
-        def _():
-            landed(carry.at[d, j, pl.ds(0, (nx - 1) * wx), :], r_xout.at[n])
-
-        if n == final - 1:
-            send_x(final, *chunks[final], core != 0)
+        def come(ref, sem):
+            @pl.when(starting)
+            def _():
+                for o in xs:
+                    carry[d, j, rows_of(o, wx), :] = jnp.zeros((wx, DV), F32)
+
+            pl.when(jnp.logical_not(starting))(lambda: landed(ref, sem))
+
+        if n == final:
+            size = wx // 2
+            for part in range(2):
+                come(carry.at[d, j, pl.ds(0, (nx - 1) * size), :], r_tail if part else r_xout.at[n])
+                for o in xs:
+                    start = pl.multiple_of(o * wx + part * size, size)
+                    send_back(n, d, j, pl.ds(start, size))
+        else:
+            come(carry.at[d, j, pl.ds(0, (nx - 1) * wx), :], r_xout.at[n])
+            if n == final - 1:
+                send_x(final, *chunks[final], 0, core != 0)
+            send_back(n, d, j, pl.ds(0, DK))
+        outer(d, mine + j)
+
+    def send_back(n, d, j, part):
         near = first if d == 0 else jnp.logical_not(first)
 
         @pl.when(near)
         def _():
-            got = carry[d, j]
-            back_buf[d, j] = d_core[mine + j] * got + total_buf[d, mine + j]
-            from_buf[d, mine + j] = got
+            got = carry[d, j, part, :]
+            back_buf[d, j, part, :] = d_core[mine + j] * got + total_buf[d, mine + j, part, :]
+            from_buf[d, mine + j, part, :] = got
 
         @pl.when(jnp.logical_not(near))
         def _():
-            got = carry[d, j]
-            back_buf[d, j] = got
-            from_buf[d, mine + j] = d_mate[mine + j] * got + peer_buf[d, j]
-
-        go(back_buf.at[d, j], from_buf.at[d, mine + j], s_back, r_back.at[n], mate)
-        outer(d, mine + j)
+            got = carry[d, j, part, :]
+            back_buf[d, j, part, :] = got
+            from_buf[d, mine + j, part, :] = d_mate[mine + j] * got + peer_buf[d, j, part, :]
+
+        go(back_buf.at[d, j, part, :], from_buf.at[d, mine + j, part, :], s_back, r_back.at[n], mate)
 
     def finish(n, d, j):
         landed(from_buf.at[d, theirs + j], r_back.at[n])
@@ -425,24 +476,24 @@
 
     def load_more(k):
         for head in (theirs + k, mine + k):
-            load(head, 0, k + 3)
-            load(head, 1, k + 3)
+            load(head, 0, k + 2)
+            load(head, 1, k + 2)
 
     def greet_mate():
         go(d_core, d_mate, s_d, r_d.at[0], mate)
         send_core(0, *chunks[0])
 
     totals = (forward_total, reverse_total)
-    ready(0, 0)
+    ready(0, 2, 1)
     forward_total(theirs)
     hear(0, 1 + CORES * (nx + ny - 2))
     pl.when(core == 0)(greet_mate)
-    ready(0, 2)
+    ready(2, 2, 1)
     forward_total(mine)
     learn(0)
     pl.when(core != 0)(greet_mate)
     load_more(1)
-    ready(0, 1)
+    ready(1, 4, 1)
     reverse_total(theirs)
     send_core(1, *chunks[1])
     landed(d_mate, r_d.at[0])
@@ -452,7 +503,6 @@
     join_cores(0, *chunks[0])
     for k in range(2, half):
         load_more(k)
-    ready(0, 3)
     reverse_total(mine)
     join_cores(1, *chunks[1])
     late, held = [], {0}
@@ -460,7 +510,7 @@
         for n in turn:
             d, k = chunks[n]
             if k not in held:
-                ready(k, k + 3)
+                ready(k + 2, 4, CORES)
                 held.add(k)
             totals[d](theirs + k)
             send_core(n, d, k)
@@ -481,8 +531,8 @@
     climb = [(2 + level, functools.partial(over_z, level)) for level in range(levels - 1)]
     top = 2 + len(climb)
     back = len(chunks)
-    stages = [(0, up_x), (0, inside), (top + 2, down_y), (back + 2, finish), (back, down_x)]
-    stages += [(1, up_y)] + climb + [(top, down_z)]
+    stages = [(0, up_x), (0, inside), (top + 3, down_y), (back + 2, finish), (back, down_x)]
+    stages += [(1, up_y)] + climb + [(top + 1, down_z)]
     for slot in range(2 * len(chunks) + 1):
         for lag, stage in stages:
             n = slot - lag
@@ -491,6 +541,7 @@
             if 0 <= n < len(chunks):
                 stage(n, *chunks[n])
             if stage is finish and n == final - 2:
+                send_x(final, *chunks[final], 1, core != 0)
                 finish(final - 1, *chunks[final - 1])
 
     left(peer_buf, s_core)
@@ -567,9 +618,9 @@
             states(max(2 * levels, nz), half, wy), states(max(1, levels - 1), 2, half, wy), states(2, half, wy),
             states(ny, 2, half, wy), states(2, half, wx),
             states(nx, 2, half, wx), states(2, half, DK),
-            decays(2 + nx + ny + nz), decays(max(1, levels), 2), pltpu.SemaphoreType.REGULAR, dma, dma((half + 3,)),
-            dma, dma((n,)), dma((nx,)), dma, dma((n,)), dma, dma((n,)), dma, dma((max(1, levels), n)),
-            dma, dma((n,)), dma((2,)), dma((n,)), dma, dma((n,)), dma, dma((4,)),
+            decays(2 + nx + ny + nz), decays(max(1, levels), 2), pltpu.SemaphoreType.REGULAR, dma, dma((half + 2,)),
+            dma, dma((half,)), dma((nx,)), dma, dma((n,)), dma, dma((n,)), dma, dma((max(1, levels - 1), n)),
+            dma, dma((n,)), dma((2,)), dma((n,)), dma, dma, dma((n,)), dma, dma((4,)),
         ],
         compiler_params=pltpu.CompilerParams(collective_id=0, has_side_effects=True, vmem_limit_bytes=52 << 20),
         name="retention",

time: 55.5 us -> 55.3 us (level)
  no operation moved by 1% of the time
where the time goes in v6:
time: 55.3 us; the launch traced here: 55.1 us
  Pallas kernels  54.5 us (99%)
  between operations  0.64 us (1%)
    pallas_call x1, Pallas kernels, body(): pl.pallas_call(functools.partial(retention_kernel, nx, ny, nz), out_shape...  52.8 us
    pallas_call x1, Pallas kernels, body(): pl.pallas_call(write_kernel, out_shape=(out, out, out), in_specs=[vm] * 3...  1.69 us

profile of v6, /device:TPU:29, one launch (start us, length us, event | category | flops | bytes accessed | tf_op | source)
XLA Modules:
  0.0 55.1 jit_solution(8004542309176989994)
XLA Ops:
  0.6 52.8 %retention.1 = (bf16[256,2048]{1,0:T(8,128)(2,1)S(1)}, bf16[256,2048]{1,0:T(8,128)(2,1)S(1)}, bf16[256,2048]{1,0:T(8,128)(2,1)S(1)}) custom-call(f32[8,256]{1,0:T(8,128)} %logs_hbm.1, bf16[256,2048]{1,0:T(8,128)(2,1)} %q_hbm.1, bf16[256,2048]{1,0:T(8,128)(2,1)} %k_hbm.1, bf16[256,2048]{1,0:T(8,128)(2,1)} %v_hbm.1, bf16[256,2048]{1,0:T(8,128)(2,1)} %g_hbm.1), custom_call_target="tpu_custom_call" | custom-call | tf_op jit(solution)/shard_map/retention/pallas_call | solution.py:603
  53.4 1.7 %write.1 = (bf16[256,2048]{1,0:T(8,128)(2,1)}, bf16[256,2048]{1,0:T(8,128)(2,1)}, bf16[256,2048]{1,0:T(8,128)(2,1)}) custom-call(bf16[256,2048]{1,0:T(8,128)(2,1)S(1)} %get-tuple-element.6.gq_ref, bf16[256,2048]{1,0:T(8,128)(2,1)S(1)} %get-tuple-element.7.gk_ref, bf16[256,2048]{1,0:T(8,128)(2,1)S(1)} %get-tuple-element.8.gv_ref), custom_call_target="tpu_custom_call" | custom-call | tf_op jit(solution)/shard_map/write/pallas_call | solution.py:628

commit v7 on v6

--- a/solution.py
+++ b/solution.py
@@ -415,6 +415,9 @@
             )
             pl.when(jnp.logical_and(jnp.logical_not(starts(d, o)), ready))(c.start)
 
+    held_late = jnp.logical_and(core != 0, starts(1, x))
+    held_soon = jnp.logical_and(core != 0, jnp.logical_not(starts(1, x)))
+
     def down_y(n, d, j):
         if ny > 1:
             landed(row_carry.at[d, j, pl.ds(0, (ny - 1) * wy), :], r_yout.at[n])
@@ -449,7 +452,7 @@
         else:
             come(carry.at[d, j, pl.ds(0, (nx - 1) * wx), :], r_xout.at[n])
             if n == final - 1:
-                send_x(final, *chunks[final], 0, core != 0)
+                send_x(final, *chunks[final], 0, held_soon)
             send_back(n, d, j, pl.ds(0, DK))
         outer(d, mine + j)
 
@@ -541,8 +544,10 @@
             if 0 <= n < len(chunks):
                 stage(n, *chunks[n])
             if stage is finish and n == final - 2:
-                send_x(final, *chunks[final], 1, core != 0)
+                send_x(final, *chunks[final], 0, held_late)
+                send_x(final, *chunks[final], 1, held_soon)
                 finish(final - 1, *chunks[final - 1])
+                send_x(final, *chunks[final], 1, held_late)
 
     left(peer_buf, s_core)
     left(x_in.at[pl.ds(0, nx - 1)], s_x)

time: 55.3 us -> 55.3 us (level)
  no operation moved by 1% of the time
where the time goes in v7:
time: 55.3 us; the launch traced here: 55.1 us
  Pallas kernels  54.5 us (99%)
  between operations  0.64 us (1%)
    pallas_call x1, Pallas kernels, body(): pl.pallas_call(functools.partial(retention_kernel, nx, ny, nz), out_shape...  52.8 us
    pallas_call x1, Pallas kernels, body(): pl.pallas_call(write_kernel, out_shape=(out, out, out), in_specs=[vm] * 3...  1.69 us

profile of v7, /device:TPU:29, one launch (start us, length us, event | category | flops | bytes accessed | tf_op | source)
XLA Modules:
  0.0 55.1 jit_solution(15452247057974768304)
XLA Ops:
  0.6 52.8 %retention.1 = (bf16[256,2048]{1,0:T(8,128)(2,1)S(1)}, bf16[256,2048]{1,0:T(8,128)(2,1)S(1)}, bf16[256,2048]{1,0:T(8,128)(2,1)S(1)}) custom-call(f32[8,256]{1,0:T(8,128)} %logs_hbm.1, bf16[256,2048]{1,0:T(8,128)(2,1)} %q_hbm.1, bf16[256,2048]{1,0:T(8,128)(2,1)} %k_hbm.1, bf16[256,2048]{1,0:T(8,128)(2,1)} %v_hbm.1, bf16[256,2048]{1,0:T(8,128)(2,1)} %g_hbm.1), custom_call_target="tpu_custom_call" | custom-call | tf_op jit(solution)/shard_map/retention/pallas_call | solution.py:608
  53.4 1.7 %write.1 = (bf16[256,2048]{1,0:T(8,128)(2,1)}, bf16[256,2048]{1,0:T(8,128)(2,1)}, bf16[256,2048]{1,0:T(8,128)(2,1)}) custom-call(bf16[256,2048]{1,0:T(8,128)(2,1)S(1)} %get-tuple-element.6.gq_ref, bf16[256,2048]{1,0:T(8,128)(2,1)S(1)} %get-tuple-element.7.gk_ref, bf16[256,2048]{1,0:T(8,128)(2,1)S(1)} %get-tuple-element.8.gv_ref), custom_call_target="tpu_custom_call" | custom-call | tf_op jit(solution)/shard_map/write/pallas_call | solution.py:633

commit v8 on v6

--- a/solution.py
+++ b/solution.py
@@ -197,23 +197,29 @@
             inner[1, head, tokens_of(b), :] = dot(wg, q, 0, 0)
             inner[2, head, tokens_of(b), :] = dot(wv, g, 0, 0)
 
-    def outer(d, head):
+    def outer(d, head, arrive=None):
+        spreads = []
+        for b in members(d, count):
+            _, cols, end = factors(head, b)
+            spreads.append((jnp.exp(cols if d == 0 else end - cols), jnp.exp(end)))
+        if arrive is not None:
+            arrive()
         coming = from_buf[d, head]
         weight = None
         for step, b in enumerate(members(d, count)):
-            _, cols, end = factors(head, b)
+            reach, last = spreads[step]
             if step == 0:
                 low = coming.astype(BF16)
             else:
                 low = (local[d, b - 1 if d == 0 else b, head] + weight * coming).astype(BF16)
-            whole = jnp.broadcast_to(jnp.exp(end), (1, DV))
+            whole = jnp.broadcast_to(last, (1, DV))
             weight = whole if weight is None else weight * whole
             if d == 0:
-                far = wide(jnp.exp(cols), DK) * dot(tok(GRADS, head, b), low, 1, 1)
+                far = wide(reach, DK) * dot(tok(GRADS, head, b), low, 1, 1)
                 near = inner[0, head, tokens_of(b), :]
                 gq_ref[tokens_of(b), cols_of(head, DK)] = (scale * (near + far)).astype(BF16)
             else:
-                tail = wide(jnp.exp(end - cols), DK)
+                tail = wide(reach, DK)
                 near = inner[1, head, tokens_of(b), :]
                 far = tail * dot(tok(VALUES, head, b), low, 1, 1)
                 gk_ref[tokens_of(b), cols_of(head, DK)] = (scale * (near + far)).astype(BF16)
@@ -471,8 +477,7 @@
         go(back_buf.at[d, j, part, :], from_buf.at[d, mine + j, part, :], s_back, r_back.at[n], mate)
 
     def finish(n, d, j):
-        landed(from_buf.at[d, theirs + j], r_back.at[n])
-        outer(d, theirs + j)
+        outer(d, theirs + j, lambda: landed(from_buf.at[d, theirs + j], r_back.at[n]))
 
     def load_more(k):
         for head in (theirs + k, mine + k):

time: 55.3 us -> 55.3 us (level)
  no operation moved by 1% of the time
where the time goes in v8:
time: 55.3 us; the launch traced here: 55.1 us
  Pallas kernels  54.5 us (99%)
  between operations  0.64 us (1%)
    pallas_call x1, Pallas kernels, body(): pl.pallas_call(functools.partial(retention_kernel, nx, ny, nz), out_shape...  52.8 us
    pallas_call x1, Pallas kernels, body(): pl.pallas_call(write_kernel, out_shape=(out, out, out), in_specs=[vm] * 3...  1.69 us

profile of v8, /device:TPU:29, one launch (start us, length us, event | category | flops | bytes accessed | tf_op | source)
XLA Modules:
  0.0 55.1 jit_solution(13113068148729927801)
XLA Ops:
  0.6 52.8 %retention.1 = (bf16[256,2048]{1,0:T(8,128)(2,1)S(1)}, bf16[256,2048]{1,0:T(8,128)(2,1)S(1)}, bf16[256,2048]{1,0:T(8,128)(2,1)S(1)}) custom-call(f32[8,256]{1,0:T(8,128)} %logs_hbm.1, bf16[256,2048]{1,0:T(8,128)(2,1)} %q_hbm.1, bf16[256,2048]{1,0:T(8,128)(2,1)} %k_hbm.1, bf16[256,2048]{1,0:T(8,128)(2,1)} %v_hbm.1, bf16[256,2048]{1,0:T(8,128)(2,1)} %g_hbm.1), custom_call_target="tpu_custom_call" | custom-call | tf_op jit(solution)/shard_map/retention/pallas_call | solution.py:608
  53.4 1.7 %write.1 = (bf16[256,2048]{1,0:T(8,128)(2,1)}, bf16[256,2048]{1,0:T(8,128)(2,1)}, bf16[256,2048]{1,0:T(8,128)(2,1)}) custom-call(bf16[256,2048]{1,0:T(8,128)(2,1)S(1)} %get-tuple-element.6.gq_ref, bf16[256,2048]{1,0:T(8,128)(2,1)S(1)} %get-tuple-element.7.gk_ref, bf16[256,2048]{1,0:T(8,128)(2,1)S(1)} %get-tuple-element.8.gv_ref), custom_call_target="tpu_custom_call" | custom-call | tf_op jit(solution)/shard_map/write/pallas_call | solution.py:633
